TPU v7x, 128 devices: a whole 4x4x4 slice. The times are simulated.
128 devices in a mesh: dp: 4 (over z), mp: 32 (over y, x, core).
Axes of the slice: x: 4, y: 4, z: 4, core: 2. Of those that a mesh axis runs over, the one named last changes fastest.
Arguments:
- tokens: bfloat16 [4096, 4096], P('dp', 'mp'), may hold values from -6 to 6
- decay: float32 [4096, 16], P('dp'), may hold values from 0.75 to 1, as said below
- state: float32 [128, 256, 8192], P('dp', None, 'mp'), may hold values from -24 to 24
- w_query: bfloat16 [4096, 4096], P(None, 'mp'), may hold values from -0.09375 to 0.09375
- w_key: bfloat16 [4096, 4096], P(None, 'mp'), may hold values from -0.09375 to 0.09375
- w_value: bfloat16 [4096, 8192], P(None, 'mp'), may hold values from -0.09375 to 0.09375
- w_gate: bfloat16 [4096, 8192], P(None, 'mp'), may hold values from -0.09375 to 0.09375
- w_out: bfloat16 [8192, 4096], P('mp'), may hold values from -0.125 to 0.125
- norm_gain: float32 [8192], P('mp'), may hold values from 0.25 to 1.75
Outputs:
- layer_out: bfloat16 [4096, 4096], P('dp', 'mp')
- new_state: float32 [128, 256, 8192], P('dp', None, 'mp')
Inputs may be any that keep to these rules, and one draw needn't show every extreme that they name: `decay`: each head has its own base rate over all tokens, varied somewhat from token to token.
All inputs are finite; a program needn't handle non-finite values.
Results may differ from a plain program's by a relative error of at most 0.0071.
Values may be sent and summed in bfloat16 or wider, within the bound.
A program may use at most 128 MiB of HBM per device.

v0:
```python
import jax
import jax.numpy as jnp
from jax import lax
from jax.sharding import PartitionSpec as P

HEAD = 256
VHEAD = 512
NEW = 32


EPS = 0.1


def partner(shard, axis, bit):
    return lax.ppermute(shard, axis, [(i, i ^ 1 << bit) for i in range(lax.axis_size(axis))])


def per_device(tokens, decay, state, w_query, w_key, w_value, w_gate, w_out, norm_gain):
    tok_rows = tokens.shape[0]
    qk_columns = w_query.shape[1]
    v_columns = w_value.shape[1]
    groups = max(1, qk_columns // HEAD)
    qk_width = qk_columns // groups
    v_width = v_columns // groups
    sequences = tok_rows // NEW
    device_index = lax.axis_index("mp")
    first_head = device_index * qk_columns // HEAD
    qk_zeros = jnp.zeros((tok_rows, qk_columns), jnp.float32)
    v_zeros = jnp.zeros((tok_rows, v_columns), jnp.float32)
    carried = (qk_zeros, qk_zeros, v_zeros, v_zeros)
    segment = lax.all_gather(tokens, "mp", axis=1, tiled=True)
    updated = []
    for running, weight in zip(carried, (w_query, w_key, w_value, w_gate)):
        weight_rows = weight
        updated.append(jnp.dot(segment, weight_rows, preferred_element_type=jnp.float32))
    query, key_proj, value_proj, gate_proj = tuple(updated)
    query = (query * HEAD ** (-0.5)).astype(jnp.bfloat16).reshape(tok_rows, groups, qk_width)
    key_proj = key_proj.astype(jnp.bfloat16).reshape(tok_rows, groups, qk_width)
    value_proj = value_proj.astype(jnp.bfloat16)
    bit_number = 0
    other_query, other_key = partner((query, key_proj), "mp", bit_number)
    upper_half = device_index >> bit_number & 1 == 1
    query = jnp.where(
        upper_half,
        jnp.concatenate([other_query, query], 2),
        jnp.concatenate([query, other_query], 2),
    )
    key_proj = jnp.where(
        upper_half,
        jnp.concatenate([other_key, key_proj], 2),
        jnp.concatenate([key_proj, other_key], 2),
    )
    query_block = query.reshape(sequences, NEW, groups, HEAD)
    key_block = key_proj.reshape(sequences, NEW, groups, HEAD)
    value_block = value_proj.reshape(sequences, NEW, groups, v_width)
    decay_rates = lax.dynamic_slice_in_dim(decay, first_head, groups, 1).reshape(
        sequences, NEW, groups
    )
    log_cumul = jnp.cumsum(jnp.log(decay_rates), axis=1)
    old_state = state.reshape(sequences, HEAD, groups, v_width)
    from_state = jnp.einsum("bngk,bkgv->bngv", query_block.astype(jnp.float32), old_state)
    scores = jnp.einsum(
        "bngk,bmgk->bgnm", query_block, key_block, preferred_element_type=jnp.float32
    )
    along = jnp.transpose(log_cumul, (0, 2, 1))
    log_gap = along[:, :, :, None] - along[:, :, None, :]
    causal = jnp.arange(NEW)[:, None] >= jnp.arange(NEW)[None, :]
    factor = jnp.where(causal, jnp.exp(jnp.where(causal, log_gap, 0.0)), 0.0)
    weights = (scores * factor).astype(jnp.bfloat16)
    in_block = jnp.einsum(
        "bgnm,bmgv->bngv", weights, value_block, preferred_element_type=jnp.float32
    )
    retained = jnp.exp(log_cumul)[..., None] * from_state + in_block
    final_log = log_cumul[:, -1, :]
    carry_scale = jnp.exp(final_log[:, None, :] - log_cumul)
    decayed_keys = key_block.astype(jnp.float32) * carry_scale[..., None]
    fresh = jnp.einsum("bngk,bngv->bkgv", decayed_keys, value_block.astype(jnp.float32))
    new_state = jnp.exp(final_log)[:, None, :, None] * old_state + fresh
    new_state = new_state.reshape(sequences, HEAD, v_columns)
    retained = retained.reshape(tok_rows, groups, v_width)
    running = jnp.sum(retained, axis=-1)
    squares = jnp.sum(retained * retained, axis=-1)
    bit_number = 0
    other_sum, other_square = partner((running, squares), "mp", bit_number)
    running = running + other_sum
    squares = squares + other_square
    centre = running / VHEAD
    variance = squares / VHEAD - centre * centre
    deviation = retained - centre[..., None]
    normed = deviation * lax.rsqrt(variance + EPS)[..., None]
    gated_out = (normed.reshape(tok_rows, v_columns) * norm_gain * jax.nn.silu(gate_proj)).astype(
        jnp.bfloat16
    )
    out_cols = lax.all_to_all(w_out, "mp", split_axis=1, concat_axis=0, tiled=True)
    weight_rows = out_cols
    layer_out = jnp.dot(
        lax.all_gather(gated_out, "mp", axis=1, tiled=True),
        weight_rows,
        preferred_element_type=jnp.float32,
    ).astype(jnp.bfloat16)
    return (layer_out, new_state)


def solution(mesh):
    placed = (
        P("dp", "mp"),
        P("dp", None),
        P("dp", None, "mp"),
        P(None, "mp"),
        P(None, "mp"),
        P(None, "mp"),
        P(None, "mp"),
        P("mp", None),
        P("mp"),
    )
    return jax.shard_map(
        per_device,
        mesh=mesh,
        in_specs=placed,
        out_specs=(P("dp", "mp"), P("dp", None, "mp")),
        check_vma=False,
    )
```

profile of v0, /device:TPU:0, one launch (start us, length us, event | category | flops | bytes accessed | tf_op | source)
XLA Modules:
  0.0 215.3 jit_solution(17912909884485674575)
XLA Ops:
  7.2 0.7 all-gather.3.cloned.1.call-update
  8.0 0.8 log_reduce_fusion
  8.8 0.5 copy.22
  9.4 2.0 fusion.26
  11.4 0.4 copy.23
  11.7 0.1 slice_reduce_fusion
  11.9 0.1 subtract_exponential_fusion
  11.9 59.4 %all-gather.3.cloned.1.call-done = bf16[1024,4096]{1,0:T(8,128)(2,1)} async-done(((bf16[1024,128]{1,0:T(8,128)(2,1)}), bf16[1024,4096]{1,0:T(8,128)(2,1)}) %all-gather.3.cloned.1.call-update) | async-done | bytes 8388624 | tf_op jit(solution)/shard_map/all_gather | solution.py:31
  71.3 6.1 %fusion.4 = bf16[1024,128]{1,0:T(8,128)(2,1)S(1)} fusion(bf16[1024,4096]{1,0:T(8,128)(2,1)} %all-gather.3.cloned.1.call-done, bf16[4096,128]{1,0:T(8,128)(2,1)} %param.12), kind=kOutput, calls=%fused_computation.11 | convolution fusion | flops 1074003968 | bytes 9699328 | tf_op jit(solution)/shard_map/dot_general | solution.py:35
  77.4 0.3 collective-permute-start
  77.8 2.3 %convolution_convert_fusion.2 = bf16[1024,128]{1,0:T(8,128)(2,1)S(1)} fusion(bf16[1024,4096]{1,0:T(8,128)(2,1)S(1)} %copy-done.10, bf16[4096,128]{1,0:T(8,128)(2,1)S(1)} %copy-done.11), kind=kOutput, calls=%fused_computation.12 | convolution fusion | flops 1073872896 | bytes 9699328 | tf_op jit(solution)/shard_map/dot_general | solution.py:35
  80.1 0.3 collective-permute-start.1
  80.4 2.3 %convolution_convert_fusion = bf16[1024,256]{1,0:T(8,128)(2,1)S(1)} fusion(bf16[1024,4096]{1,0:T(8,128)(2,1)S(1)} %copy-done.10, bf16[4096,256]{1,0:T(8,128)(2,1)S(1)} %copy-done), kind=kOutput, calls=%fused_computation.6 | convolution fusion | flops 2147745792 | bytes 11010048 | tf_op jit(solution)/shard_map/dot_general | solution.py:35
  82.8 0.8 copy-done.8
  83.6 1.5 convolution_bitcast_fusion
  85.2 4.5 %fusion.9 = (f32[32,32]{1,0:T(8,128)S(1)}, f32[32,32]{1,0:T(8,128)S(1)}, f32[32,1,256,32]{2,3,0,1:T(8,128)S(1)}) fusion(f32[32,1,256,32]{2,3,0,1:T(8,128)S(1)} %convolution_bitcast_fusion, f32[32,256,256]{2,1,0:T(8,128)} %param.11, bf16[32,32,128]{2,1,0:T(8,128)(2,1)S(1)} %bitcast.72, bf16[32,32,128]{2,1,0:T(8,128)(2,1)} %bitcast.74, pred[]{:T(512)S(6)} %eq.3, ...), kind=kOutput, calls=%fused_computation.20 | convolution fusion | flops 137885696 | bytes 11022337 | tf_op jit(solution)/shard_map/bngk,bkgv->bngv/dot_general | solution.py:61
  89.7 0.1 reduce_sum.25
  89.8 0.1 reduce_sum.23
  89.9 0.3 collective-permute-start.2
  90.2 0.3 collective-permute-start.3
  90.4 0.7 collective-permute-done.2
  91.1 0.2 collective-permute-done.3
  91.4 7.4 %fusion.8 = bf16[1024,256]{1,0:T(8,128)(2,1)} fusion(f32[32,1,256,32]{2,3,0,1:T(8,128)S(1)} %get-tuple-element.14, f32[256]{0:T(256)S(1)} %copy-done.12, f32[1024]{0:T(1024)S(1)} %bitcast.81, f32[1024]{0:T(1024)S(1)} %bitcast.82, bf16[1024,4096]{1,0:T(8,128)(2,1)} %all-gather.3.cloned.1.call-done, bf16[4096,256]{1,0:T(8,128)(2,1)} %param.15), kind=kOutput, calls=%fused_computation.17 | convolution fusion | flops 2149842944 | bytes 12067840 | tf_op jit(solution)/shard_map/dot_general | solution.py:35
  98.8 2.5 %copy.24 = bf16[256,4096]{0,1:T(8,128)(2,1)} copy(bf16[256,4096]{1,0:T(8,128)(2,1)S(1)} %copy-done.2) | data formatting | bytes 4194304 | tf_op args[7]
  101.3 5.8 %all-to-all-start = ((bf16[256,32,128]{0,2,1:T(8,128)(2,1)}), bf16[256,32,128]{0,2,1:T(8,128)(2,1)S(1)}, u32[]{:S(2)}, u32[]{:S(2)}) async-start(bf16[256,32,128]{0,2,1:T(8,128)(2,1)} %bitcast.66), calls=%async_computation | async-start | bytes 4194304 | tf_op jit(solution)/shard_map/all_to_all | solution.py:94
  107.1 9.2 %copy.26 = f32[32,256,256]{1,2,0:T(8,128)} copy(f32[32,256,256]{2,1,0:T(8,128)} %param.11) | data formatting | bytes 16777216 | tf_op args[2]
  116.3 27.6 %all-to-all-done = bf16[256,32,128]{0,2,1:T(8,128)(2,1)S(1)} async-done(((bf16[256,32,128]{0,2,1:T(8,128)(2,1)}), bf16[256,32,128]{0,2,1:T(8,128)(2,1)S(1)}, u32[]{:S(2)}, u32[]{:S(2)}) %all-to-all-start) | async-done | bytes 2097184 | tf_op jit(solution)/shard_map/all_to_all | solution.py:94
  143.9 2.9 %copy.25 = bf16[32,256,128]{2,1,0:T(8,128)(2,1)} copy(bf16[32,256,128]{1,2,0:T(8,128)(2,1)S(1)} %bitcast.65) | data formatting | bytes 4194304 | tf_op jit(solution)/shard_map/all_to_all | solution.py:94
  146.8 8.5 %fusion = f32[32,256,256]{1,2,0:T(8,128)} fusion(f32[32,256,256]{1,2,0:T(8,128)} %copy.26, f32[32]{0:T(128)S(1)} %exp.38, bf16[32,32,256]{2,1,0:T(8,128)(2,1)S(1)} %bitcast.69, f32[32,32]{1,0:T(8,128)S(1)} %get-tuple-element.12, bf16[32,32,128]{2,1,0:T(8,128)(2,1)S(1)} %bitcast.77, bf16[32,32,128]{2,1,0:T(8,128)(2,1)S(1)} %bitcast.79, pred[]{:T(512)S(6)} %eq.3), kind=kOutput, calls=%fused_computation.1 | convolution fusion | flops 141295616 | bytes 17830016 | tf_op jit(solution)/shard_map/bngk,bngv->bkgv/dot_general | solution.py:77
  155.4 9.0 %copy.27 = f32[32,256,256]{2,1,0:T(8,128)} copy(f32[32,256,256]{1,2,0:T(8,128)} %fusion) | data formatting | bytes 16777216
  164.4 32.4 %all-gather.5.cloned.1.call-done = bf16[1024,8192]{1,0:T(8,128)(2,1)} async-done(((bf16[1024,256]{1,0:T(8,128)(2,1)}), bf16[1024,8192]{1,0:T(8,128)(2,1)}) %all-gather.5.cloned.1.call-update) | async-done | bytes 16777232 | tf_op jit(solution)/shard_map/all_gather | solution.py:97
  196.8 11.7 %convolution_convert_fusion.1 = bf16[1024,128]{1,0:T(8,128)(2,1)} fusion(bf16[1024,8192]{1,0:T(8,128)(2,1)} %all-gather.5.cloned.1.call-done, bf16[8192,128]{1,0:T(8,128)(2,1)} %bitcast.67), kind=kOutput, calls=%fused_computation.9 | convolution fusion | flops 2147614720 | bytes 19136512 | tf_op jit(solution)/shard_map/dot_general | solution.py:96
  (34 shorter events, 0.3 us)
Async XLA Ops:
  7.2 73.3 %copy-start = (bf16[4096,256]{1,0:T(8,128)(2,1)S(1)}, bf16[4096,256]{1,0:T(8,128)(2,1)}, u32[]{:S(2)}) copy-start(bf16[4096,256]{1,0:T(8,128)(2,1)} %param.14) | copy-start | bytes 6291460
  7.2 64.2 %all-gather.3.cloned.1.call-start = ((), (), s32[]{:S(2)}) async-start(), calls=%async_computation.1 | async-start | bytes 8650752 | tf_op jit(solution)/shard_map/all_gather | solution.py:31
  7.9 188.9 %all-gather.5.cloned.1.call-start = ((), (), s32[]{:S(2)}) async-start(), calls=%async_computation.2 | async-start | bytes 17301504 | tf_op jit(solution)/shard_map/all_gather | solution.py:97
  71.3 6.4 %copy-start.10 = (bf16[1024,4096]{1,0:T(8,128)(2,1)S(1)}, bf16[1024,4096]{1,0:T(8,128)(2,1)}, u32[]{:S(2)}) copy-start(bf16[1024,4096]{1,0:T(8,128)(2,1)} %all-gather.3.cloned.1.call-done) | copy-start | bytes 25165828
  71.3 6.4 %copy-start.11 = (bf16[4096,128]{1,0:T(8,128)(2,1)S(1)}, bf16[4096,128]{1,0:T(8,128)(2,1)}, u32[]{:S(2)}) copy-start(bf16[4096,128]{1,0:T(8,128)(2,1)} %param.13) | copy-start | bytes 3145732
  77.4 5.4 %collective-permute-start = (bf16[1024,1,128]{2,0,1:T(8,128)(2,1)S(1)}, bf16[1024,1,128]{2,0,1:T(8,128)(2,1)S(1)}, u32[]{:S(2)}, u32[]{:S(2)}) collective-permute-start(bf16[1024,1,128]{2,0,1:T(8,128)(2,1)S(1)} %bitcast.70), channel_id=1, source_target_pairs={{0,1},{1,0},{2,3},{3,2},{4,5},{5,4},{6,7},{7,6},{8,9},{9,8},{10,11... | collective-permute-start | bytes 786440 | tf_op jit(solution)/shard_map/ppermute | solution.py:15
  80.1 5.1 %copy-start.6 = (bf16[1024,128]{1,0:T(8,128)(2,1)}, bf16[1024,128]{1,0:T(8,128)(2,1)S(1)}, u32[]{:S(2)}) copy-start(bf16[1024,128]{1,0:T(8,128)(2,1)S(1)} %convolution_convert_fusion.2) | copy-start | bytes 786436
  80.1 2.7 %collective-permute-start.1 = (bf16[1024,1,128]{2,0,1:T(8,128)(2,1)S(1)}, bf16[1024,1,128]{2,0,1:T(8,128)(2,1)S(1)}, u32[]{:S(2)}, u32[]{:S(2)}) collective-permute-start(bf16[1024,1,128]{2,0,1:T(8,128)(2,1)S(1)} %bitcast.75), channel_id=1, source_target_pairs={{0,1},{1,0},{2,3},{3,2},{4,5},{5,4},{6,7},{7,6},{8,9},{9,8},{10,11... | collective-permute-start | bytes 786440 | tf_op jit(solution)/shard_map/ppermute | solution.py:15
  82.8 2.4 %copy-start.3 = (bf16[1024,256]{1,0:T(8,128)(2,1)}, bf16[1024,256]{1,0:T(8,128)(2,1)S(1)}, u32[]{:S(2)}) copy-start(bf16[1024,256]{1,0:T(8,128)(2,1)S(1)} %convolution_convert_fusion) | copy-start | bytes 1572868
  82.8 2.4 %copy-start.5 = (bf16[1024,1,128]{2,0,1:T(8,128)(2,1)}, bf16[1024,1,128]{2,0,1:T(8,128)(2,1)S(1)}, u32[]{:S(2)}) copy-start(bf16[1024,1,128]{2,0,1:T(8,128)(2,1)S(1)} %collective-permute-done) | copy-start | bytes 786436
  82.8 0.8 copy-start.8
  83.6 7.7 %copy-start.12 = (f32[256]{0:T(256)S(1)}, f32[256]{0:T(256)}, u32[]{:S(2)}) copy-start(f32[256]{0:T(256)} %param.17) | copy-start | bytes 3076
  89.9 1.2 collective-permute-start.2
  90.2 1.2 collective-permute-start.3
  91.4 7.4 %copy-start.2 = (bf16[256,4096]{1,0:T(8,128)(2,1)S(1)}, bf16[256,4096]{1,0:T(8,128)(2,1)}, u32[]{:S(2)}) copy-start(bf16[256,4096]{1,0:T(8,128)(2,1)} %param.16) | copy-start | bytes 6291460
  101.3 42.6 %all-to-all-start = ((bf16[256,32,128]{0,2,1:T(8,128)(2,1)}), bf16[256,32,128]{0,2,1:T(8,128)(2,1)S(1)}, u32[]{:S(2)}, u32[]{:S(2)}) async-start(bf16[256,32,128]{0,2,1:T(8,128)(2,1)} %bitcast.66), calls=%async_computation | async-start | bytes 4194304 | tf_op jit(solution)/shard_map/all_to_all | solution.py:94
  107.0 39.8 %copy-start.4 = (bf16[1024,256]{1,0:T(8,128)(2,1)S(1)}, bf16[1024,256]{1,0:T(8,128)(2,1)}, u32[]{:S(2)}) copy-start(bf16[1024,256]{1,0:T(8,128)(2,1)} %copy-done.3) | copy-start | bytes 1572868
  107.1 39.8 %copy-start.7 = (bf16[1024,128]{1,0:T(8,128)(2,1)S(1)}, bf16[1024,128]{1,0:T(8,128)(2,1)}, u32[]{:S(2)}) copy-start(bf16[1024,128]{1,0:T(8,128)(2,1)} %copy-done.6) | copy-start | bytes 786436
  107.1 39.8 %copy-start.9 = (bf16[1024,1,128]{2,0,1:T(8,128)(2,1)S(1)}, bf16[1024,1,128]{2,0,1:T(8,128)(2,1)}, u32[]{:S(2)}) copy-start(bf16[1024,1,128]{2,0,1:T(8,128)(2,1)} %copy-done.8) | copy-start | bytes 786436
  196.8 11.7 %copy-start.1 = (bf16[4096,256]{1,0:T(8,128)(2,1)S(1)}, bf16[4096,256]{1,0:T(8,128)(2,1)}, u32[]{:S(2)}) copy-start(bf16[4096,256]{1,0:T(8,128)(2,1)} %param.14) | copy-start | bytes 6291460
Sparse Core Ops, SparseCore 0:
  10.2 61.1 all-gather.2
  98.9 97.8 all-gather.4
where the time goes:
time: 217 us; the launch traced here: 215 us
  waiting for transfers between devices  121 us (56%)
  matrix products  44.5 us (21%)
  local copies, waits for them, and re-layouts  26.4 us (12%)
  between operations  14.3 us (7%)
  starting transfers between devices  7.03 us (3%)
    all_gather x1, waiting for transfers between devices, per_device(): segment = lax.all_gather(tokens, 'mp', axis=1, tiled=True)  59.4 us
    all_gather x1, waiting for transfers between devices, per_device(): lax.all_gather(gated_out, 'mp', axis=1, tiled=True)  32.4 us
    all_to_all x1, waiting for transfers between devices, per_device(): lax.all_to_all(w_out, 'mp', split_axis=1, concat_axis=0, tiled=True)  27.6 us
    unnamed x29, local copies, waits for them, and re-layouts  21.5 us
    dot_general x4, matrix products, per_device(): jnp.dot(segment, weight_rows, preferred_element_type=jnp.float32)  18.2 us
    dot_general x1, matrix products, per_device(): jnp.dot(lax.all_gather(gated_out, 'mp', axis=1, tiled=True), weight_rows,...  11.7 us
    dot_general x1, matrix products, per_device(): jnp.einsum('bngk,bngv->bkgv', decayed_keys, value_block.astype(jnp.float32))  8.54 us
    all_to_all x1, starting transfers between devices, per_device(): lax.all_to_all(w_out, 'mp', split_axis=1, concat_axis=0, tiled=True)  5.76 us
  transfers between devices with their start and end apart: 7, of which 5 were waited for; matrix products, arithmetic and copies ran while one was open for 19% of the time, Pallas kernels for 0%

commit v1 on v0

v1 whole, which is shorter than its diff:
```python
import functools

import jax
import jax.numpy as jnp
from jax import lax
from jax.experimental import pallas as pl
from jax.experimental.pallas import tpu as pltpu
from jax.sharding import PartitionSpec as P

HEAD = 256
VHEAD = 512
NEW = 32
EPS = 0.1
SIDE = 4
CHIPS = SIDE * SIDE
BLOCK = 128

MESH = pl.DeviceIdType.MESH
HIGHEST = lax.Precision.HIGHEST
BF16 = jnp.bfloat16
F32 = jnp.float32


class Place:
    def __init__(self):
        self.me = lax.axis_index("mp")
        self.core = lax.rem(self.me, 2)
        chip = lax.div(self.me, 2)
        y, x = lax.div(chip, SIDE), lax.rem(chip, SIDE)
        self.a = x * (1 - self.core) + y * self.core
        self.b = y * (1 - self.core) + x * self.core
        self.step_a = 1 + (SIDE - 1) * self.core
        self.step_b = SIDE - (SIDE - 1) * self.core
        self.partner = self.me + 1 - 2 * self.core

    def chip(self, da, db):
        a = lax.rem(self.a + (da + SIDE), SIDE)
        b = lax.rem(self.b + (db + SIDE), SIDE)
        return a * self.step_a + b * self.step_b

    def at(self, da, db):
        return self.chip(da, db) * 2 + self.core

    def partner_at(self, da, db):
        a = lax.rem(self.b + (da + SIDE), SIDE)
        b = lax.rem(self.a + (db + SIDE), SIDE)
        return (a * self.step_b + b * self.step_a) * 2 + 1 - self.core


def remote(src, dst, send_sem, recv_sem, device):
    return pltpu.make_async_remote_copy(
        src_ref=src,
        dst_ref=dst,
        send_sem=send_sem,
        recv_sem=recv_sem,
        device_id={"mp": device},
        device_id_type=MESH,
    )


def greet(place):
    barrier = pltpu.get_barrier_semaphore()
    others = (place.partner, place.at(1, 0), place.at(-1, 0), place.at(0, 1), place.at(0, -1))
    for other in others:
        pl.semaphore_signal(barrier, inc=1, device_id={"mp": other}, device_id_type=MESH)
    pl.semaphore_wait(barrier, len(others))


ARRIVALS = (
    ((-1, 0, 0), (1, 0, 0), (0, -1, 0), (0, 1, 0)),
    ((-1, 0, 1), (1, 0, 1)),
    ((0, -1, 1), (0, 1, 1)),
    ((-1, -1, 0), (-1, 1, 0), (1, -1, 0), (1, 1, 0), (2, 0, 0), (2, 0, 1), (0, 2, 0), (0, 2, 1)),
    ((-1, -1, 1), (-1, 1, 1)),
    ((1, -1, 1), (1, 1, 1)),
    ((2, -1, 0), (2, 1, 0), (2, -1, 1), (2, 1, 1)),
    ((-1, 2, 0), (-1, 2, 1), (1, 2, 0), (1, 2, 1)),
    ((2, 2, 0), (2, 2, 1)),
)
PAIRS = {
    1: ((-1, 0), (1, 0)),
    2: ((0, -1), (0, 1)),
    3: ((2, 0), (0, 2)),
    4: ((-1, -1), (-1, 1)),
    5: ((1, -1), (1, 1)),
    6: ((2, -1), (2, 1)),
    7: ((-1, 2), (1, 2)),
}


def gather_kernel(
    tokens, w_query, w_key, w_value, w_gate, w_out,
    query, key_proj, value_proj, gate_proj, other_out,
    held, weights, total, send_sems, recv_sems, side_sems, local_sems,
):
    place = Place()
    rows = tokens.shape[0]
    sub = rows // 2
    me, core, partner = place.me, place.core, place.partner
    sent = []

    def rows_of(half):
        return pl.ds(half * sub, sub)

    def send(src, block, half, device):
        copy = remote(
            src, held.at[block, rows_of(half)], send_sems.at[len(sent)], recv_sems.at[block, half], device
        )
        copy.start()
        sent.append(copy)

    greet(place)
    ring = (place.at(1, 0), place.at(-1, 0), place.at(0, 1), place.at(0, -1))
    a_up, a_down, b_up, b_down = ring
    for half in range(2):
        for device in ring + (partner,):
            send(tokens.at[rows_of(half)], me, half, device)
    mine = pl.ds(pl.multiple_of(core * BLOCK, BLOCK), BLOCK)
    loads = [
        pltpu.make_async_copy(tokens, held.at[me], local_sems.at[0]),
        pltpu.make_async_copy(w_query, weights.at[0, :, mine], local_sems.at[1]),
        pltpu.make_async_copy(w_key, weights.at[1, :, mine], local_sems.at[2]),
        pltpu.make_async_copy(w_value, weights.at[2], local_sems.at[3]),
        pltpu.make_async_copy(w_gate, weights.at[3], local_sems.at[4]),
    ]
    for load in loads:
        load.start()
    exchanged = [
        remote(w_query, weights.at[0, :, mine], side_sems.at[0], side_sems.at[1], partner),
        remote(w_key, weights.at[1, :, mine], side_sems.at[2], side_sems.at[3], partner),
    ]
    for copy in exchanged:
        copy.start()
    for chip in range(CHIPS):
        columns = pl.ds(pl.multiple_of(chip * 2 * BLOCK + (1 - core) * BLOCK, BLOCK), BLOCK)
        remote(
            w_out.at[:, columns], other_out.at[chip], side_sems.at[4], side_sems.at[5], partner
        ).start()

    def wait_for(block, half):
        slot = held.at[block, rows_of(half)]
        remote(slot, slot, send_sems.at[0], recv_sems.at[block, half], partner).wait_recv()

    def arrive(da, db, half):
        block = place.at(da, db)
        wait_for(block, half)
        slot = held.at[block, rows_of(half)]
        if db == 0:
            if (da, half) == (-1, 0):
                send(slot, block, half, a_up)
            if (da, half) == (1, 1):
                send(slot, block, half, a_down)
            send(slot, block, half, b_up)
            send(slot, block, half, b_down)
        elif (db, half) == (-1, 0):
            send(slot, block, half, b_up)
        elif (db, half) == (1, 1):
            send(slot, block, half, b_down)
        send(slot, block, half, partner)

    def project(first, second, begin=False):
        def body(index, carry):
            which, half = lax.div(index, 2), lax.rem(index, 2)
            span = pl.ds(pl.multiple_of(half * sub, sub), sub)
            left = jnp.concatenate([held[first, span, :], held[second, span, :]], axis=1)
            right = jnp.concatenate(
                [
                    weights[which, pl.ds(pl.multiple_of(first * BLOCK, BLOCK), BLOCK), :],
                    weights[which, pl.ds(pl.multiple_of(second * BLOCK, BLOCK), BLOCK), :],
                ],
                axis=0,
            )
            part = jnp.dot(left, right, preferred_element_type=F32)
            if begin:
                total[which, span, :] = part
            else:
                total[which, span, :] += part
            return carry

        lax.fori_loop(0, 8, body, 0)

    def partner_pair(pair):
        blocks = [place.partner_at(*offset) for offset in pair]
        for block in blocks:
            for half in range(2):
                wait_for(block, half)
        project(*blocks)

    for stage, events in enumerate(ARRIVALS):
        for event in events:
            arrive(*event)
        if stage == 0:
            for load in loads:
                load.wait()
            for copy in exchanged:
                copy.wait()
            wait_for(partner, 0)
            wait_for(partner, 1)
            project(me, partner, begin=True)
        if stage in PAIRS:
            project(*[place.at(*offset) for offset in PAIRS[stage]])
        if stage - 1 in PAIRS:
            partner_pair(PAIRS[stage - 1])
    far, partner_far = place.at(2, 2), place.partner_at(2, 2)
    for half in range(2):
        wait_for(partner_far, half)
    project(far, partner_far)

    def finish(index, carry):
        span = pl.ds(pl.multiple_of(index * (rows // 8), rows // 8), rows // 8)
        query[span, :] = (total[0, span, :] * HEAD ** (-0.5)).astype(BF16)
        key_proj[span, :] = total[1, span, :].astype(BF16)
        value_proj[span, :] = total[2, span, :].astype(BF16)
        gate_proj[span, :] = total[3, span, :]
        return carry

    lax.fori_loop(0, 8, finish, 0)
    remote(other_out, other_out, side_sems.at[4], side_sems.at[5], partner).wait()
    for copy in sent:
        copy.wait_send()


def gather_and_project(tokens, w_query, w_key, w_value, w_gate, w_out):
    rows, features = tokens.shape[0], w_query.shape[0]
    half_flops = 2 * rows * features * 1024
    anywhere = pl.BlockSpec(memory_space=pl.ANY)
    inside = pl.BlockSpec(memory_space=pltpu.VMEM)
    return pl.pallas_call(
        gather_kernel,
        out_shape=(
            jax.ShapeDtypeStruct((rows, HEAD), BF16),
            jax.ShapeDtypeStruct((rows, HEAD), BF16),
            jax.ShapeDtypeStruct((rows, 256), BF16),
            jax.ShapeDtypeStruct((rows, 256), F32),
            jax.ShapeDtypeStruct((CHIPS, 256, BLOCK), BF16),
        ),
        in_specs=[anywhere] * 6,
        out_specs=(inside, inside, inside, inside, anywhere),
        scratch_shapes=[
            pltpu.VMEM((2 * CHIPS, rows, BLOCK), BF16),
            pltpu.VMEM((4, features, 256), BF16),
            pltpu.VMEM((4, rows, 256), F32),
            pltpu.SemaphoreType.DMA((64,)),
            pltpu.SemaphoreType.DMA((2 * CHIPS, 2)),
            pltpu.SemaphoreType.DMA((6,)),
            pltpu.SemaphoreType.DMA((5,)),
        ],
        compiler_params=pltpu.CompilerParams(
            collective_id=0, has_side_effects=True, vmem_limit_bytes=40 * 2**20
        ),
        cost_estimate=pl.CostEstimate(flops=half_flops, bytes_accessed=2**24, transcendentals=0),
        name="gather_project",
    )(tokens, w_query, w_key, w_value, w_gate, w_out)


def retention_kernel(
    query, key_proj, value_proj, gate_proj, decay, gain, state, new_state, retained, scale, stats
):
    head = lax.div(lax.axis_index("mp"), 2)
    rows = query.shape[0]
    sequences = rows // NEW
    rates = jnp.log(decay[...])
    lane = lax.broadcasted_iota(jnp.int32, rates.shape, 1)
    rate = jnp.sum(jnp.where(lane == head, rates, 0.0), axis=1, keepdims=True)
    rate = jnp.broadcast_to(rate, (rows, 128))
    to = lax.broadcasted_iota(jnp.int32, (rows, rows), 0)
    at = lax.broadcasted_iota(jnp.int32, (rows, rows), 1)
    same = lax.div(to, NEW) == lax.div(at, NEW)
    causal = jnp.logical_and(same, at <= to)
    cumul = jnp.dot(causal.astype(F32), rate, precision=HIGHEST, preferred_element_type=F32)
    final = jnp.dot(same.astype(F32), rate, precision=HIGHEST, preferred_element_type=F32)
    pick = (lax.broadcasted_iota(jnp.int32, (8, 128), 1) == 0).astype(F32)
    along = lax.dot_general(
        pick, cumul, (((1,), (1,)), ((), ())), precision=HIGHEST, preferred_element_type=F32
    )[:1, :]
    wide = jnp.concatenate([cumul] * (rows // 128), axis=1) if rows > 128 else cumul[:, :rows]
    gap = jnp.where(causal, wide - along, 0.0)
    factor = jnp.where(causal, jnp.exp(gap), 0.0)
    q, k, v = query[...], key_proj[...], value_proj[...]
    scores = lax.dot_general(q, k, (((1,), (1,)), ((), ())), preferred_element_type=F32)
    weights = (scores * factor).astype(BF16)
    in_block = jnp.dot(weights, v, preferred_element_type=F32)
    carry_scale = jnp.exp(final - cumul)
    decayed = (k.astype(F32) * jnp.concatenate([carry_scale] * 2, axis=1)).astype(BF16)
    from_scale = jnp.exp(cumul)
    from_scale = jnp.concatenate([from_scale] * 2, axis=1)
    final_scale = jnp.exp(final)
    final_scale = jnp.concatenate([final_scale] * 2, axis=1)
    for s in range(sequences):
        span = slice(s * NEW, (s + 1) * NEW)
        old = state[s]
        from_state = jnp.dot(q[span], old.astype(BF16), preferred_element_type=F32)
        retained[span, :] = from_scale[span] * from_state + in_block[span]
        fresh = lax.dot_general(
            decayed[span], v[span], (((0,), (0,)), ((), ())), preferred_element_type=F32
        )
        new_state[s] = final_scale[s * NEW : s * NEW + 1] * old + fresh
    values = retained[...]
    first = jnp.sum(values, axis=1, keepdims=True)
    second = jnp.sum(values * values, axis=1, keepdims=True)
    lanes = lax.broadcasted_iota(jnp.int32, (rows, 128), 1)
    stats[...] = jnp.where(lanes < 64, first, second)
    g = gate_proj[...]
    scale[...] = gain[...] * (g / (1.0 + jnp.exp(-g)))


def retention(query, key_proj, value_proj, gate_proj, decay, gain, state):
    rows = query.shape[0]
    tile = min(rows, 256)
    sequences = tile // NEW
    block = pl.BlockSpec((tile, 256), lambda i: (i, 0))
    return pl.pallas_call(
        retention_kernel,
        grid=(rows // tile,),
        out_shape=(
            jax.ShapeDtypeStruct(state.shape, F32),
            jax.ShapeDtypeStruct((rows, 256), F32),
            jax.ShapeDtypeStruct((rows, 256), F32),
            jax.ShapeDtypeStruct((rows, 128), F32),
        ),
        in_specs=[
            block,
            block,
            block,
            block,
            pl.BlockSpec((tile, decay.shape[1]), lambda i: (i, 0)),
            pl.BlockSpec((1, 256), lambda i: (0, 0)),
            pl.BlockSpec((sequences, 256, 256), lambda i: (i, 0, 0)),
        ],
        out_specs=(
            pl.BlockSpec((sequences, 256, 256), lambda i: (i, 0, 0)),
            block,
            block,
            pl.BlockSpec((tile, 128), lambda i: (i, 0)),
        ),
        compiler_params=pltpu.CompilerParams(vmem_limit_bytes=32 * 2**20),
        name="retention",
    )(query, key_proj, value_proj, gate_proj, decay, gain.reshape(1, -1), state)


ORDER = (2, 1, -1, 0)


def reduce_kernel(
    retained, scale, stats, w_out, other_out,
    layer_out,
    other_stats, gated, out_rows, s1, r1, s2, r2, column_sum,
    pair_sems, ss1, rs1, ss2, rs2, local_sems,
):
    place = Place()
    rows = retained.shape[0]
    sub = rows // 2
    core, partner = place.core, place.partner
    sent = []

    greet(place)
    exchange = remote(stats, other_stats, pair_sems.at[0], pair_sems.at[1], partner)
    exchange.start()
    loads = []
    own_rows = pl.ds(pl.multiple_of(core * 256, 256), 256)
    other_rows = pl.ds(pl.multiple_of((1 - core) * 256, 256), 256)
    for chip in range(CHIPS):
        columns = pl.ds(pl.multiple_of(chip * 2 * BLOCK + core * BLOCK, BLOCK), BLOCK)
        loads.append(
            pltpu.make_async_copy(w_out.at[:, columns], out_rows.at[chip, own_rows], local_sems.at[chip])
        )
    loads.append(pltpu.make_async_copy(other_out, out_rows.at[:, other_rows], local_sems.at[CHIPS]))
    for load in loads:
        load.start()
    exchange.wait_recv()
    tile = min(sub, 256)
    for half in range(2):
        def gate(index, carry):
            span = pl.ds(pl.multiple_of(half * sub + index * tile, tile), tile)
            both = stats[span, :] + other_stats[span, :]
            centre = both[:, :1] / VHEAD
            variance = both[:, 64:65] / VHEAD - centre * centre
            inverse = lax.rsqrt(variance + EPS)
            gated[core, span, :] = (
                (retained[span, :] - centre) * inverse * scale[span, :]
            ).astype(BF16)
            return carry

        lax.fori_loop(0, sub // tile, gate, 0)
        slot = gated.at[core, pl.ds(half * sub, sub)]
        copy = remote(slot, slot, pair_sems.at[2 + 2 * half], pair_sems.at[3 + 2 * half], partner)
        copy.start()
        sent.append(copy)
    for load in loads:
        load.wait()
    for half in range(2):
        slot = gated.at[1 - core, pl.ds(half * sub, sub)]
        remote(slot, slot, pair_sems.at[2 + 2 * half], pair_sems.at[3 + 2 * half], partner).wait_recv()

    def part(da, db, half):
        chip = place.chip(da, db)
        span = pl.ds(half * sub, sub)
        return jnp.dot(
            gated[0, span, :], out_rows[chip, :256, :], preferred_element_type=F32
        ) + jnp.dot(gated[1, span, :], out_rows[chip, 256:, :], preferred_element_type=F32)

    b_next = (place.at(0, 1), place.at(0, -1))
    a_next = (place.at(1, 0), place.at(-1, 0))

    def put1(way, kind, j, value):
        s1[way, kind, j] = value.astype(BF16)
        copy = remote(
            s1.at[way, kind, j], r1.at[way, kind, j], ss1.at[way, kind, j], rs1.at[way, kind, j], b_next[way]
        )
        copy.start()
        sent.append(copy)

    def got1(way, kind, j):
        remote(
            s1.at[way, kind, j], r1.at[way, kind, j], ss1.at[way, kind, j], rs1.at[way, kind, j], b_next[way]
        ).wait_recv()
        return r1[way, kind, j].astype(F32)

    def put2(way, kind, value):
        s2[way, kind] = value.astype(BF16)
        copy = remote(s2.at[way, kind], r2.at[way, kind], ss2.at[way, kind], rs2.at[way, kind], a_next[way])
        copy.start()
        sent.append(copy)

    def got2(way, kind):
        remote(
            s2.at[way, kind], r2.at[way, kind], ss2.at[way, kind], rs2.at[way, kind], a_next[way]
        ).wait_recv()
        return r2[way, kind].astype(F32)

    def far1(j):
        for way in range(2):
            put1(way, 0, j, part(ORDER[j], 2, way))

    def plain1(j):
        for way in range(2):
            put1(way, 1, j, part(ORDER[j], 1 - 2 * way, 1 - way))

    def sum1(j):
        for way in range(2):
            mine = part(ORDER[j], 1 - 2 * way, way)
            put1(way, 2, j, mine + got1(way, 0, j))

    def column(j, half):
        mine = part(ORDER[j], 0, half)
        return mine + got1(half, 2, j) + got1(1 - half, 1, j)

    far1(0)
    far1(1)
    plain1(0)
    sum1(0)
    far1(2)
    plain1(1)
    sum1(1)
    for half in range(2):
        put2(half, 0, column(0, half))
    far1(3)
    plain1(2)
    sum1(2)
    put2(0, 1, column(1, 1))
    mine = column(1, 0)
    put2(0, 2, mine + got2(0, 0))
    plain1(3)
    sum1(3)
    put2(1, 1, column(2, 0))
    mine = column(2, 1)
    put2(1, 2, mine + got2(1, 0))
    for half in range(2):
        column_sum[pl.ds(half * sub, sub), :] = column(3, half)
    for half in range(2):
        span = pl.ds(half * sub, sub)
        layer_out[span, :] = (column_sum[span, :] + got2(half, 2) + got2(1 - half, 1)).astype(BF16)
    exchange.wait_send()
    for copy in sent:
        copy.wait_send()


def project_and_reduce(retained, scale, stats, w_out, other_out):
    rows = retained.shape[0]
    sub = rows // 2
    anywhere = pl.BlockSpec(memory_space=pl.ANY)
    inside = pl.BlockSpec(memory_space=pltpu.VMEM)
    return pl.pallas_call(
        reduce_kernel,
        out_shape=jax.ShapeDtypeStruct((rows, BLOCK), BF16),
        in_specs=[inside, inside, inside, anywhere, anywhere],
        out_specs=inside,
        scratch_shapes=[
            pltpu.VMEM((rows, 128), F32),
            pltpu.VMEM((2, rows, 256), BF16),
            pltpu.VMEM((CHIPS, 512, BLOCK), BF16),
            pltpu.VMEM((2, 3, 4, sub, BLOCK), BF16),
            pltpu.VMEM((2, 3, 4, sub, BLOCK), BF16),
            pltpu.VMEM((2, 3, sub, BLOCK), BF16),
            pltpu.VMEM((2, 3, sub, BLOCK), BF16),
            pltpu.VMEM((rows, BLOCK), F32),
            pltpu.SemaphoreType.DMA((6,)),
            pltpu.SemaphoreType.DMA((2, 3, 4)),
            pltpu.SemaphoreType.DMA((2, 3, 4)),
            pltpu.SemaphoreType.DMA((2, 3)),
            pltpu.SemaphoreType.DMA((2, 3)),
            pltpu.SemaphoreType.DMA((CHIPS + 1,)),
        ],
        compiler_params=pltpu.CompilerParams(
            collective_id=1, has_side_effects=True, vmem_limit_bytes=32 * 2**20
        ),
        cost_estimate=pl.CostEstimate(flops=2 * rows * 512 * 2048, bytes_accessed=2**23, transcendentals=0),
        name="project_reduce",
    )(retained, scale, stats, w_out, other_out)


def per_device(tokens, decay, state, w_query, w_key, w_value, w_gate, w_out, norm_gain):
    query, key_proj, value_proj, gate_proj, other_out = gather_and_project(
        tokens, w_query, w_key, w_value, w_gate, w_out
    )
    new_state, retained, scale, stats = retention(
        query, key_proj, value_proj, gate_proj, decay, norm_gain, state
    )
    layer_out = project_and_reduce(retained, scale, stats, w_out, other_out)
    return layer_out, new_state


def solution(mesh):
    placed = (
        P("dp", "mp"),
        P("dp", None),
        P("dp", None, "mp"),
        P(None, "mp"),
        P(None, "mp"),
        P(None, "mp"),
        P(None, "mp"),
        P("mp", None),
        P("mp"),
    )
    return jax.shard_map(
        per_device,
        mesh=mesh,
        in_specs=placed,
        out_specs=(P("dp", "mp"), P("dp", None, "mp")),
        check_vma=False,
    )
```

time: 217 us -> 100 us (0.46)
  waiting for transfers between devices: 121 us -> 0 us
  Pallas kernels: 0 us -> 86 us
  matrix products: 44.5 us -> 0 us
  between operations: 14.3 us -> 0.68 us
  local copies, waits for them, and re-layouts: 26.4 us -> 13.3 us
  starting transfers between devices: 7.03 us -> 0 us
    all_gather x2 -> x0, waiting for transfers between devices: 91.8 us -> none  [the longest x1 59.4 us: per_device(): segment = lax.all_gather(tokens, 'mp', axis=1, tiled=True)]
    pallas_call x0 -> x3, Pallas kernels: none -> 86 us  [the longest x1 44 us: gather_and_project(): pl.pallas_call(gather_kernel, out_shape=(jax.ShapeDtypeStruct((rows, HEAD...]
    dot_general x8 -> x0, matrix products: 44.5 us -> none  [the longest x4 18.2 us: per_device(): jnp.dot(segment, weight_rows, preferred_element_type=jnp.float32)]
    all_to_all x1 -> x0, waiting for transfers between devices: 27.6 us -> none  [per_device(): lax.all_to_all(w_out, 'mp', split_axis=1, concat_axis=0, tiled=True)]
    unnamed x29 -> x18, local copies, waits for them, and re-layouts: 21.5 us -> 13.3 us
    all_to_all x1 -> x0, starting transfers between devices: 5.76 us -> none  [per_device(): lax.all_to_all(w_out, 'mp', split_axis=1, concat_axis=0, tiled=True)]
    all_to_all x1 -> x0, local copies, waits for them, and re-layouts: 2.92 us -> none  [per_device(): lax.all_to_all(w_out, 'mp', split_axis=1, concat_axis=0, tiled=True)]
  transfers between devices with their start and end apart: 7 -> 0, of which waited for: 5 -> 0; matrix products, arithmetic and copies ran while one was open for 19% -> 0% of each run, Pallas kernels for 0% -> 0%
where the time goes in v1:
time: 100 us
  Pallas kernels  86 us (86%)
  local copies, waits for them, and re-layouts  13.3 us (13%)
    pallas_call x1, Pallas kernels, gather_and_project(): pl.pallas_call(gather_kernel, out_shape=(jax.ShapeDtypeStruct((rows, HEAD...  44 us
    pallas_call x1, Pallas kernels, project_and_reduce(): pl.pallas_call(reduce_kernel, out_shape=jax.ShapeDtypeStruct((rows, BLOCK...  34.4 us
    unnamed x18, local copies, waits for them, and re-layouts  13.3 us
    pallas_call x1, Pallas kernels, retention(): pl.pallas_call(retention_kernel, grid=(rows // tile,), out_shape=(jax.Sha...  7.6 us

profile of v1, /device:TPU:0, one launch (start us, length us, event | category | flops | bytes accessed | tf_op | source)
XLA Modules:
  0.0 100.0 jit_solution(11815147371640223600)
XLA Ops:
  0.6 1.0 %copy.11.decay = f32[1024,16]{1,0:T(8,128)S(1)} copy(f32[1024,16]{0,1:T(8,128)} %param.10) | data formatting | bytes 131072 | tf_op args[1]
  1.7 0.0 copy-start.2
  1.7 1.6 %copy-done.2 = bf16[4096,256]{1,0:T(8,128)(2,1)S(1)} copy-done((bf16[4096,256]{1,0:T(8,128)(2,1)S(1)}, bf16[4096,256]{1,0:T(8,128)(2,1)}, u32[]{:S(2)}) %copy-start.2) | copy-done | bytes 2097176
  3.3 0.0 copy-start.3
  3.3 1.6 %copy-done.3 = bf16[4096,256]{1,0:T(8,128)(2,1)S(1)} copy-done((bf16[4096,256]{1,0:T(8,128)(2,1)S(1)}, bf16[4096,256]{1,0:T(8,128)(2,1)}, u32[]{:S(2)}) %copy-start.3) | copy-done | bytes 2097176
  4.9 0.0 copy-start.4
  4.9 1.6 %copy-done.4 = bf16[256,4096]{1,0:T(8,128)(2,1)S(1)} copy-done((bf16[256,4096]{1,0:T(8,128)(2,1)S(1)}, bf16[256,4096]{1,0:T(8,128)(2,1)}, u32[]{:S(2)}) %copy-start.4) | copy-done | bytes 2097176
  6.5 0.0 copy-start.5
  6.5 1.2 %copy-done.5 = bf16[4096,128]{1,0:T(8,128)(2,1)S(1)} copy-done((bf16[4096,128]{1,0:T(8,128)(2,1)S(1)}, bf16[4096,128]{1,0:T(8,128)(2,1)}, u32[]{:S(2)}) %copy-start.5) | copy-done | bytes 1048600
  7.7 0.0 copy-start.6
  7.7 1.2 %copy-done.6 = bf16[4096,128]{1,0:T(8,128)(2,1)S(1)} copy-done((bf16[4096,128]{1,0:T(8,128)(2,1)S(1)}, bf16[4096,128]{1,0:T(8,128)(2,1)}, u32[]{:S(2)}) %copy-start.6) | copy-done | bytes 1048600
  8.9 0.0 copy-start.7
  8.9 0.9 copy-done.7
  9.9 0.0 copy-start.1
  9.9 44.0 %gather_project.1 = (bf16[1024,256]{1,0:T(8,128)(2,1)S(1)}, bf16[1024,256]{1,0:T(8,128)(2,1)S(1)}, bf16[1024,256]{1,0:T(8,128)(2,1)S(1)}, f32[1024,256]{1,0:T(8,128)S(1)}, bf16[16,256,128]{2,1,0:T(8,128)(2,1)S(1)}) custom-call(bf16[1024,128]{1,0:T(8,128)(2,1)S(1)} %copy-done.7, bf16[4096,128]{1,0:T(8,128)(2,1)S(1)} %copy-done.5, ...), custom_call_target="tpu_custom_call" | custom-call | flops 8589934592 | bytes 16777216 | tf_op jit(solution)/shard_map/gather_project/pallas_call | solution.py:228
  53.9 0.0 copy-done.1
  53.9 0.0 copy-start
  53.9 3.4 %copy-done = f32[32,256,256]{2,1,0:T(8,128)S(1)} copy-done((f32[32,256,256]{2,1,0:T(8,128)S(1)}, f32[32,256,256]{2,1,0:T(8,128)}, u32[]{:S(2)}) %copy-start) | copy-done | bytes 8388632
  57.3 7.6 %retention.1 = (f32[32,256,256]{2,1,0:T(8,128)}, f32[1024,256]{1,0:T(8,128)S(1)}, f32[1024,256]{1,0:T(8,128)S(1)}, f32[1024,128]{1,0:T(8,128)S(1)}) custom-call(bf16[1024,256]{1,0:T(8,128)(2,1)S(1)} %get-tuple-element.11.query, bf16[1024,256]{1,0:T(8,128)(2,1)S(1)} %get-tuple-element.12.key_proj, bf16[1024,256]{1,0:T(8,128)(2,1)S(1)} %get-tuple-element.13.value_proj, ...), custom_call_target="tpu_custom_call" | custom-call | tf_op jit(solution)/shard_map/retention/pallas_call | solution.py:312
  64.9 34.4 %project_reduce.1 = bf16[1024,128]{1,0:T(8,128)(2,1)S(1)} custom-call(f32[1024,256]{1,0:T(8,128)S(1)} %get-tuple-element.15.retained, f32[1024,256]{1,0:T(8,128)S(1)} %get-tuple-element.16.scale, f32[1024,128]{1,0:T(8,128)S(1)} %get-tuple-element.17.stats, bf16[256,4096]{1,0:T(8,128)(2,1)S(1)} %copy-done.4, bf16[16,256,128]{2,1,0:T(8,128)(2,1)S(1)} %get-tuple-element.18.other_out), custom_call_target="tpu_custom_call" | custom-call | flops 2147483648 | bytes 8388608 | tf_op jit(solution)/shard_map/project_reduce/pallas_call | solution.py:483
  99.3 0.7 copy.13
Async XLA Ops:
  1.7 1.6 %copy-start.2 = (bf16[4096,256]{1,0:T(8,128)(2,1)S(1)}, bf16[4096,256]{1,0:T(8,128)(2,1)}, u32[]{:S(2)}) copy-start(bf16[4096,256]{1,0:T(8,128)(2,1)} %w_value.1) | copy-start | bytes 6291460
  3.3 1.6 %copy-start.3 = (bf16[4096,256]{1,0:T(8,128)(2,1)S(1)}, bf16[4096,256]{1,0:T(8,128)(2,1)}, u32[]{:S(2)}) copy-start(bf16[4096,256]{1,0:T(8,128)(2,1)} %w_gate.1) | copy-start | bytes 6291460
  4.9 1.6 %copy-start.4 = (bf16[256,4096]{1,0:T(8,128)(2,1)S(1)}, bf16[256,4096]{1,0:T(8,128)(2,1)}, u32[]{:S(2)}) copy-start(bf16[256,4096]{1,0:T(8,128)(2,1)} %w_out.3) | copy-start | bytes 6291460
  6.5 1.2 %copy-start.5 = (bf16[4096,128]{1,0:T(8,128)(2,1)S(1)}, bf16[4096,128]{1,0:T(8,128)(2,1)}, u32[]{:S(2)}) copy-start(bf16[4096,128]{1,0:T(8,128)(2,1)} %w_query.1) | copy-start | bytes 3145732
  7.7 1.2 %copy-start.6 = (bf16[4096,128]{1,0:T(8,128)(2,1)S(1)}, bf16[4096,128]{1,0:T(8,128)(2,1)}, u32[]{:S(2)}) copy-start(bf16[4096,128]{1,0:T(8,128)(2,1)} %w_key.1) | copy-start | bytes 3145732
  8.9 0.9 copy-start.7
  9.9 44.0 %copy-start.1 = (f32[256]{0:T(256)S(1)}, f32[256]{0:T(256)}, u32[]{:S(2)}) copy-start(f32[256]{0:T(256)} %param.17) | copy-start | bytes 3076
  53.9 3.4 %copy-start = (f32[32,256,256]{2,1,0:T(8,128)S(1)}, f32[32,256,256]{2,1,0:T(8,128)}, u32[]{:S(2)}) copy-start(f32[32,256,256]{2,1,0:T(8,128)} %state.1) | copy-start | bytes 25165828

commit v2 on v1

--- a/solution.py
+++ b/solution.py
@@ -11,6 +11,8 @@
 VHEAD = 512
 NEW = 32
 EPS = 0.1
+TILE = 512
+UNROLL = 8
 SIDE = 4
 CHIPS = SIDE * SIDE
 BLOCK = 128
@@ -158,18 +160,14 @@
             send(slot, block, half, b_down)
         send(slot, block, half, partner)
 
-    def project(first, second, begin=False):
+    def project(*blocks, begin=False):
+        starts = [pl.multiple_of(block * BLOCK, BLOCK) for block in blocks]
+
         def body(index, carry):
-            which, half = lax.div(index, 2), lax.rem(index, 2)
-            span = pl.ds(pl.multiple_of(half * sub, sub), sub)
-            left = jnp.concatenate([held[first, span, :], held[second, span, :]], axis=1)
-            right = jnp.concatenate(
-                [
-                    weights[which, pl.ds(pl.multiple_of(first * BLOCK, BLOCK), BLOCK), :],
-                    weights[which, pl.ds(pl.multiple_of(second * BLOCK, BLOCK), BLOCK), :],
-                ],
-                axis=0,
-            )
+            which, tile = lax.div(index, rows // TILE), lax.rem(index, rows // TILE)
+            span = pl.ds(pl.multiple_of(tile * TILE, TILE), TILE)
+            left = jnp.concatenate([held[block, span, :] for block in blocks], axis=1)
+            right = jnp.concatenate([weights[which, pl.ds(start, BLOCK), :] for start in starts], axis=0)
             part = jnp.dot(left, right, preferred_element_type=F32)
             if begin:
                 total[which, span, :] = part
@@ -177,14 +175,7 @@
                 total[which, span, :] += part
             return carry
 
-        lax.fori_loop(0, 8, body, 0)
-
-    def partner_pair(pair):
-        blocks = [place.partner_at(*offset) for offset in pair]
-        for block in blocks:
-            for half in range(2):
-                wait_for(block, half)
-        project(*blocks)
+        lax.fori_loop(0, 4 * (rows // TILE), body, 0, unroll=UNROLL)
 
     for stage, events in enumerate(ARRIVALS):
         for event in events:
@@ -197,10 +188,12 @@
             wait_for(partner, 0)
             wait_for(partner, 1)
             project(me, partner, begin=True)
-        if stage in PAIRS:
-            project(*[place.at(*offset) for offset in PAIRS[stage]])
         if stage - 1 in PAIRS:
-            partner_pair(PAIRS[stage - 1])
+            theirs = [place.partner_at(*offset) for offset in PAIRS[stage - 1]]
+            for block in theirs:
+                for half in range(2):
+                    wait_for(block, half)
+            project(*[place.at(*offset) for offset in PAIRS[stage - 1]], *theirs)
     far, partner_far = place.at(2, 2), place.partner_at(2, 2)
     for half in range(2):
         wait_for(partner_far, half)
@@ -223,7 +216,7 @@
 def gather_and_project(tokens, w_query, w_key, w_value, w_gate, w_out):
     rows, features = tokens.shape[0], w_query.shape[0]
     half_flops = 2 * rows * features * 1024
-    anywhere = pl.BlockSpec(memory_space=pl.ANY)
+    anywhere = pl.BlockSpec(memory_space=pltpu.HBM)
     inside = pl.BlockSpec(memory_space=pltpu.VMEM)
     return pl.pallas_call(
         gather_kernel,
@@ -333,7 +326,7 @@
             block,
             pl.BlockSpec((tile, 128), lambda i: (i, 0)),
         ),
-        compiler_params=pltpu.CompilerParams(vmem_limit_bytes=32 * 2**20),
+        compiler_params=pltpu.CompilerParams(vmem_limit_bytes=60 * 2**20),
         name="retention",
     )(query, key_proj, value_proj, gate_proj, decay, gain.reshape(1, -1), state)
 
@@ -478,7 +471,7 @@
 def project_and_reduce(retained, scale, stats, w_out, other_out):
     rows = retained.shape[0]
     sub = rows // 2
-    anywhere = pl.BlockSpec(memory_space=pl.ANY)
+    anywhere = pl.BlockSpec(memory_space=pltpu.HBM)
     inside = pl.BlockSpec(memory_space=pltpu.VMEM)
     return pl.pallas_call(
         reduce_kernel,

time: 100 us -> 97.5 us (0.975)
  Pallas kernels: 86 us -> 78.7 us
  local copies, waits for them, and re-layouts: 13.3 us -> 17.6 us
    pallas_call x1, Pallas kernels: 44 us -> 33.7 us  [gather_and_project(): pl.pallas_call(gather_kernel, out_shape=(jax.ShapeDtypeStruct((rows, HEAD...]
    unnamed x18 -> x30, local copies, waits for them, and re-layouts: 13.3 us -> 17.6 us
    pallas_call x1, Pallas kernels: 7.6 us -> 11.7 us  [retention(): pl.pallas_call(retention_kernel, grid=(rows // tile,), out_shape=(jax.Sha...]
    pallas_call x1, Pallas kernels: 34.4 us -> 33.4 us  [project_and_reduce(): pl.pallas_call(reduce_kernel, out_shape=jax.ShapeDtypeStruct((rows, BLOCK...]
where the time goes in v2:
time: 97.5 us; the launch traced here: 97 us
  Pallas kernels  78.7 us (81%)
  local copies, waits for them, and re-layouts  17.6 us (18%)
    pallas_call x1, Pallas kernels, gather_and_project(): pl.pallas_call(gather_kernel, out_shape=(jax.ShapeDtypeStruct((rows, HEAD...  33.7 us
    pallas_call x1, Pallas kernels, project_and_reduce(): pl.pallas_call(reduce_kernel, out_shape=jax.ShapeDtypeStruct((rows, BLOCK...  33.4 us
    unnamed x30, local copies, waits for them, and re-layouts  17.6 us
    pallas_call x1, Pallas kernels, retention(): pl.pallas_call(retention_kernel, grid=(rows // tile,), out_shape=(jax.Sha...  11.7 us

profile of v2, /device:TPU:0, one launch (start us, length us, event | category | flops | bytes accessed | tf_op | source)
XLA Modules:
  0.0 97.0 jit_solution(12017837353974890603)
XLA Ops:
  0.6 1.8 %copy.11.decay = f32[1024,16]{1,0:T(8,128)} copy(f32[1024,16]{0,1:T(8,128)} %param.10) | data formatting | bytes 131072 | tf_op args[1]
  2.5 0.0 copy-start.4
  2.5 1.6 %copy-done.4 = bf16[4096,256]{1,0:T(8,128)(2,1)S(1)} copy-done((bf16[4096,256]{1,0:T(8,128)(2,1)S(1)}, bf16[4096,256]{1,0:T(8,128)(2,1)}, u32[]{:S(2)}) %copy-start.4) | copy-done | bytes 2097176
  4.1 0.0 copy-start.5
  4.1 1.6 %copy-done.5 = bf16[4096,256]{1,0:T(8,128)(2,1)S(1)} copy-done((bf16[4096,256]{1,0:T(8,128)(2,1)S(1)}, bf16[4096,256]{1,0:T(8,128)(2,1)}, u32[]{:S(2)}) %copy-start.5) | copy-done | bytes 2097176
  5.7 0.0 copy-start.6
  5.7 1.6 %copy-done.6 = bf16[256,4096]{1,0:T(8,128)(2,1)S(1)} copy-done((bf16[256,4096]{1,0:T(8,128)(2,1)S(1)}, bf16[256,4096]{1,0:T(8,128)(2,1)}, u32[]{:S(2)}) %copy-start.6) | copy-done | bytes 2097176
  7.3 0.0 copy-start.8
  7.3 1.2 %copy-done.8 = bf16[4096,128]{1,0:T(8,128)(2,1)S(1)} copy-done((bf16[4096,128]{1,0:T(8,128)(2,1)S(1)}, bf16[4096,128]{1,0:T(8,128)(2,1)}, u32[]{:S(2)}) %copy-start.8) | copy-done | bytes 1048600
  8.5 0.0 copy-start.9
  8.5 1.2 %copy-done.9 = bf16[4096,128]{1,0:T(8,128)(2,1)S(1)} copy-done((bf16[4096,128]{1,0:T(8,128)(2,1)S(1)}, bf16[4096,128]{1,0:T(8,128)(2,1)}, u32[]{:S(2)}) %copy-start.9) | copy-done | bytes 1048600
  9.7 0.0 copy-start.13
  9.7 0.9 copy-done.13
  10.7 33.7 %gather_project.1 = (bf16[1024,256]{1,0:T(8,128)(2,1)S(1)}, bf16[1024,256]{1,0:T(8,128)(2,1)S(1)}, bf16[1024,256]{1,0:T(8,128)(2,1)S(1)}, f32[1024,256]{1,0:T(8,128)S(1)}, bf16[16,256,128]{2,1,0:T(8,128)(2,1)S(1)}) custom-call(bf16[1024,128]{1,0:T(8,128)(2,1)S(1)} %copy-done.13, bf16[4096,128]{1,0:T(8,128)(2,1)S(1)} %copy-done.8, ...), custom_call_target="tpu_custom_call" | custom-call | flops 8589934592 | bytes 16777216 | tf_op jit(solution)/shard_map/gather_project/pallas_call | solution.py:221
  44.3 0.0 copy-start
  44.3 1.0 %copy-done = f32[1024,256]{1,0:T(8,128)} copy-done((f32[1024,256]{1,0:T(8,128)}, f32[1024,256]{1,0:T(8,128)S(1)}, u32[]{:S(2)}) %copy-start) | copy-done | bytes 1048600
  45.3 0.0 copy-start.1
  45.3 0.8 copy-done.1
  46.1 0.0 copy-start.2
  46.1 0.8 copy-done.2
  46.9 0.0 copy-start.3
  46.9 0.8 copy-done.3
  47.7 0.0 copy-start.7
  47.7 11.7 %retention.1 = (f32[32,256,256]{2,1,0:T(8,128)}, f32[1024,256]{1,0:T(8,128)}, f32[1024,256]{1,0:T(8,128)}, f32[1024,128]{1,0:T(8,128)}) custom-call(bf16[1024,256]{1,0:T(8,128)(2,1)} %copy-done.1, bf16[1024,256]{1,0:T(8,128)(2,1)} %copy-done.2, bf16[1024,256]{1,0:T(8,128)(2,1)} %copy-done.3, f32[1024,256]{1,0:T(8,128)} %copy-done, f32[1024,16]{1,0:T(8,128)} %copy.11.decay, ...), custom_call_target="tpu_custom_call" | custom-call | tf_op jit(solution)/shard_map/retention/pallas_call | solution.py:305
  59.4 0.0 copy-done.7
  59.4 0.0 copy-start.10
  59.4 1.2 %copy-done.10 = f32[1024,256]{1,0:T(8,128)S(1)} copy-done((f32[1024,256]{1,0:T(8,128)S(1)}, f32[1024,256]{1,0:T(8,128)}, u32[]{:S(2)}) %copy-start.10) | copy-done | bytes 1048600
  60.6 0.0 copy-start.11
  60.6 1.2 %copy-done.11 = f32[1024,256]{1,0:T(8,128)S(1)} copy-done((f32[1024,256]{1,0:T(8,128)S(1)}, f32[1024,256]{1,0:T(8,128)}, u32[]{:S(2)}) %copy-start.11) | copy-done | bytes 1048600
  61.8 1.0 %copy-done.12 = f32[1024,128]{1,0:T(8,128)S(1)} copy-done((f32[1024,128]{1,0:T(8,128)S(1)}, f32[1024,128]{1,0:T(8,128)}, u32[]{:S(2)}) %copy-start.12) | copy-done | bytes 524312
  62.9 33.4 %project_reduce.1 = bf16[1024,128]{1,0:T(8,128)(2,1)S(1)} custom-call(f32[1024,256]{1,0:T(8,128)S(1)} %copy-done.10, f32[1024,256]{1,0:T(8,128)S(1)} %copy-done.11, f32[1024,128]{1,0:T(8,128)S(1)} %copy-done.12, bf16[256,4096]{1,0:T(8,128)(2,1)S(1)} %copy-done.7, bf16[16,256,128]{2,1,0:T(8,128)(2,1)S(1)} %get-tuple-element.18.other_out), custom_call_target="tpu_custom_call" | custom-call | flops 2147483648 | bytes 8388608 | tf_op jit(solution)/shard_map/project_reduce/pallas_call | solution.py:476
  96.3 0.7 copy.13
  (1 shorter events, 0.0 us)
Async XLA Ops:
  2.5 1.6 %copy-start.4 = (bf16[4096,256]{1,0:T(8,128)(2,1)S(1)}, bf16[4096,256]{1,0:T(8,128)(2,1)}, u32[]{:S(2)}) copy-start(bf16[4096,256]{1,0:T(8,128)(2,1)} %w_value.1) | copy-start | bytes 6291460
  4.1 1.6 %copy-start.5 = (bf16[4096,256]{1,0:T(8,128)(2,1)S(1)}, bf16[4096,256]{1,0:T(8,128)(2,1)}, u32[]{:S(2)}) copy-start(bf16[4096,256]{1,0:T(8,128)(2,1)} %w_gate.1) | copy-start | bytes 6291460
  5.7 1.6 %copy-start.6 = (bf16[256,4096]{1,0:T(8,128)(2,1)S(1)}, bf16[256,4096]{1,0:T(8,128)(2,1)}, u32[]{:S(2)}) copy-start(bf16[256,4096]{1,0:T(8,128)(2,1)} %w_out.3) | copy-start | bytes 6291460
  7.3 1.2 %copy-start.8 = (bf16[4096,128]{1,0:T(8,128)(2,1)S(1)}, bf16[4096,128]{1,0:T(8,128)(2,1)}, u32[]{:S(2)}) copy-start(bf16[4096,128]{1,0:T(8,128)(2,1)} %w_query.1) | copy-start | bytes 3145732
  8.5 1.2 %copy-start.9 = (bf16[4096,128]{1,0:T(8,128)(2,1)S(1)}, bf16[4096,128]{1,0:T(8,128)(2,1)}, u32[]{:S(2)}) copy-start(bf16[4096,128]{1,0:T(8,128)(2,1)} %w_key.1) | copy-start | bytes 3145732
  9.7 0.9 copy-start.13
  44.3 1.0 %copy-start = (f32[1024,256]{1,0:T(8,128)}, f32[1024,256]{1,0:T(8,128)S(1)}, u32[]{:S(2)}) copy-start(f32[1024,256]{1,0:T(8,128)S(1)} %get-tuple-element.14.gate_proj) | copy-start | bytes 3145732
  45.3 0.8 copy-start.1
  46.1 0.8 copy-start.2
  46.9 0.8 copy-start.3
  47.7 11.7 %copy-start.7 = (bf16[256,4096]{1,0:T(8,128)(2,1)S(1)}, bf16[256,4096]{1,0:T(8,128)(2,1)}, u32[]{:S(2)}) copy-start(bf16[256,4096]{1,0:T(8,128)(2,1)} %w_out.3) | copy-start | bytes 6291460
  59.4 1.2 %copy-start.10 = (f32[1024,256]{1,0:T(8,128)S(1)}, f32[1024,256]{1,0:T(8,128)}, u32[]{:S(2)}) copy-start(f32[1024,256]{1,0:T(8,128)} %get-tuple-element.15.retained) | copy-start | bytes 3145732
  60.6 1.2 %copy-start.11 = (f32[1024,256]{1,0:T(8,128)S(1)}, f32[1024,256]{1,0:T(8,128)}, u32[]{:S(2)}) copy-start(f32[1024,256]{1,0:T(8,128)} %get-tuple-element.16.scale) | copy-start | bytes 3145732
  61.8 1.0 %copy-start.12 = (f32[1024,128]{1,0:T(8,128)S(1)}, f32[1024,128]{1,0:T(8,128)}, u32[]{:S(2)}) copy-start(f32[1024,128]{1,0:T(8,128)} %get-tuple-element.17.stats) | copy-start | bytes 1572868

commit v3 on v0

v3 whole, which is shorter than its diff:
```python
import functools

import jax
import jax.numpy as jnp
from jax import lax
from jax.experimental import pallas as pl
from jax.experimental.pallas import tpu as pltpu
from jax.sharding import PartitionSpec as P

HEAD = 256
VHEAD = 512
NEW = 32
EPS = 0.1
CHUNKS = 2
STEPS = 8
VMEM_LIMIT = 62 * 2**20
SIDE = 4
CHIPS = SIDE * SIDE
BLOCK = 128

MESH = pl.DeviceIdType.MESH
HIGHEST = lax.Precision.HIGHEST
BF16 = jnp.bfloat16
F32 = jnp.float32


class Place:
    def __init__(self):
        self.me = lax.axis_index("mp")
        self.core = lax.rem(self.me, 2)
        chip = lax.div(self.me, 2)
        y, x = lax.div(chip, SIDE), lax.rem(chip, SIDE)
        self.a = x * (1 - self.core) + y * self.core
        self.b = y * (1 - self.core) + x * self.core
        self.step_a = 1 + (SIDE - 1) * self.core
        self.step_b = SIDE - (SIDE - 1) * self.core
        self.partner = self.me + 1 - 2 * self.core

    def chip(self, da, db):
        a = lax.rem(self.a + (da + SIDE), SIDE)
        b = lax.rem(self.b + (db + SIDE), SIDE)
        return a * self.step_a + b * self.step_b

    def at(self, da, db):
        return self.chip(da, db) * 2 + self.core

    def partner_at(self, da, db):
        a = lax.rem(self.b + (da + SIDE), SIDE)
        b = lax.rem(self.a + (db + SIDE), SIDE)
        return (a * self.step_b + b * self.step_a) * 2 + 1 - self.core


def remote(src, dst, send_sem, recv_sem, device):
    return pltpu.make_async_remote_copy(
        src_ref=src,
        dst_ref=dst,
        send_sem=send_sem,
        recv_sem=recv_sem,
        device_id={"mp": device},
        device_id_type=MESH,
    )


def greet(place):
    barrier = pltpu.get_barrier_semaphore()
    others = (place.partner, place.at(1, 0), place.at(-1, 0), place.at(0, 1), place.at(0, -1))
    for other in others:
        pl.semaphore_signal(barrier, inc=1, device_id={"mp": other}, device_id_type=MESH)
    pl.semaphore_wait(barrier, len(others))


ARRIVALS = (
    ((-1, 0, 0), (1, 0, 0), (0, -1, 0), (0, 1, 0)),
    ((-1, 0, 1), (1, 0, 1)),
    ((0, -1, 1), (0, 1, 1)),
    ((-1, -1, 0), (-1, 1, 0), (1, -1, 0), (1, 1, 0), (2, 0, 0), (2, 0, 1), (0, 2, 0), (0, 2, 1)),
    ((-1, -1, 1), (-1, 1, 1)),
    ((1, -1, 1), (1, 1, 1)),
    ((2, -1, 0), (2, 1, 0), (2, -1, 1), (2, 1, 1)),
    ((-1, 2, 0), (-1, 2, 1), (1, 2, 0), (1, 2, 1)),
    ((2, 2, 0), (2, 2, 1)),
)
PAIRS = {
    1: ((-1, 0), (1, 0)),
    2: ((0, -1), (0, 1)),
    3: ((2, 0), (0, 2)),
    4: ((-1, -1), (-1, 1)),
    5: ((1, -1), (1, 1)),
    6: ((2, -1), (2, 1)),
    7: ((-1, 2), (1, 2)),
}


ORDER = (2, 1, -1, 0)
GROUP = 256
PAIR_NT = (((1,), (1,)), ((), ()))
PAIR_TN = (((0,), (0,)), ((), ()))


def kernel(
    tokens, decay, gain, state, w_query, w_key, w_value, w_gate, w_out,
    layer_out, decayed_out, value_out, scale_out,
    held, old_state, decayed, values, scales, weights, total, out_rows, cumul, final, along,
    retained, stats, other_stats, gated, own1, near1, s1, r1, s2, r2, own2,
    send_sems, recv_sems, side_sems, load_sems, stat_sems, gate_sems, ss1, rs1, ss2, rs2, out_sems,
):
    place = Place()
    rows = tokens.shape[0]
    chunk = rows // CHUNKS
    sub = chunk // 2
    group = min(GROUP, chunk)
    me, core, partner = place.me, place.core, place.partner
    a_next = (place.at(1, 0), place.at(-1, 0))
    b_next = (place.at(0, 1), place.at(0, -1))
    sent, kept_copies = [], []
    counts = [0]

    greet(place)


    def rows_of(c, half):
        return pl.ds(c * chunk + half * sub, sub)

    def send(src, block, c, half, device):
        copy = remote(
            src, held.at[block, rows_of(c, half)],
            send_sems.at[counts[0]], recv_sems.at[c, block, half], device,
        )
        counts[0] += 1
        copy.start()
        sent.append(copy)

    def own(c, devices):
        for half in range(2):
            for device in devices:
                send(tokens.at[rows_of(c, half)], me, c, half, device)

    def wait_for(block, c, half):
        slot = held.at[block, rows_of(c, half)]
        remote(slot, slot, send_sems.at[0], recv_sems.at[c, block, half], partner).wait_recv()

    def arrive(c, da, db, half):
        block = place.at(da, db)
        wait_for(block, c, half)
        slot = held.at[block, rows_of(c, half)]
        if db == 0:
            if (da, half) == (-1, 0):
                send(slot, block, c, half, a_next[0])
            if (da, half) == (1, 1):
                send(slot, block, c, half, a_next[1])
            send(slot, block, c, half, b_next[0])
            send(slot, block, c, half, b_next[1])
        elif (db, half) == (-1, 0):
            send(slot, block, c, half, b_next[0])
        elif (db, half) == (1, 1):
            send(slot, block, c, half, b_next[1])
        send(slot, block, c, half, partner)

    def arrivals(c, stage):
        for event in ARRIVALS[stage]:
            arrive(c, *event)

    def project(c, step):
        if step == 0:
            theirs, blocks = [partner], [me, partner]
        elif step in PAIRS:
            theirs = [place.partner_at(*offset) for offset in PAIRS[step]]
            blocks = [place.at(*offset) for offset in PAIRS[step]] + theirs
        else:
            theirs = [place.partner_at(2, 2)]
            blocks = [place.at(2, 2)] + theirs
        for block in theirs:
            for half in range(2):
                wait_for(block, c, half)
        starts = [pl.multiple_of(block * BLOCK, BLOCK) for block in blocks]
        span = pl.ds(c * chunk, chunk)

        def body(which, carry):
            left = jnp.concatenate([held[block, span, :] for block in blocks], axis=1)
            right = jnp.concatenate([weights[which, pl.ds(start, BLOCK), :] for start in starts], axis=0)
            part = jnp.dot(left, right, preferred_element_type=F32)
            if step == 0:
                total[which, span, :] = part
            else:
                total[which, span, :] += part
            return carry

        lax.fori_loop(0, 4, body, 0, unroll=4)


    def decays():
        head = lax.div(me, 2)
        rates = jnp.log(decay[...])
        lane = lax.broadcasted_iota(jnp.int32, rates.shape, 0)
        rate = jnp.sum(jnp.where(lane == head, rates, 0.0), axis=0, keepdims=True)
        to = lax.broadcasted_iota(jnp.int32, (group, group), 0)
        at = lax.broadcasted_iota(jnp.int32, (group, group), 1)
        same = lax.div(to, NEW) == lax.div(at, NEW)
        causal = jnp.logical_and(same, at <= to).astype(F32)
        for g in range(rows // group):
            mine = rate[:, g * group : (g + 1) * group]
            mine = jnp.broadcast_to(mine, (128, group))
            span = slice(g * group, (g + 1) * group)
            cumul[span, :] = lax.dot_general(
                causal, mine, PAIR_NT, precision=HIGHEST, preferred_element_type=F32
            )
            final[span, :] = lax.dot_general(
                same.astype(F32), mine, PAIR_NT, precision=HIGHEST, preferred_element_type=F32
            )
            along[g] = lax.dot_general(
                mine[:8], causal, PAIR_NT, precision=HIGHEST, preferred_element_type=F32
            )

    def retain(g):
        span = pl.ds(g * group, group)
        query = (total[0, span, :] * HEAD ** (-0.5)).astype(BF16)
        key = total[1, span, :].astype(BF16)
        value = total[2, span, :].astype(BF16)
        to = lax.broadcasted_iota(jnp.int32, (group, group), 0)
        at = lax.broadcasted_iota(jnp.int32, (group, group), 1)
        causal = jnp.logical_and(lax.div(to, NEW) == lax.div(at, NEW), at <= to)
        c = cumul[span, :]
        wide = jnp.concatenate([c] * (group // 128), axis=1) if group > 128 else c[:, :group]
        gap = jnp.where(causal, wide - along[g, :1, :], 0.0)
        factor = jnp.where(causal, jnp.exp(gap), 0.0)
        scores = lax.dot_general(query, key, PAIR_NT, preferred_element_type=F32)
        weight = (scores * factor).astype(BF16)
        in_block = jnp.dot(weight, value, preferred_element_type=F32)
        last = final[span, :]
        carry_scale = jnp.exp(last - c)
        faded = (key.astype(F32) * jnp.concatenate([carry_scale] * 2, axis=1)).astype(BF16)
        from_scale = jnp.exp(c)
        from_scale = jnp.concatenate([from_scale] * 2, axis=1)
        last_scale = jnp.exp(last)
        last_scale = jnp.concatenate([last_scale] * 2, axis=1)
        parts = []
        for s in range(group // NEW):
            part = slice(s * NEW, (s + 1) * NEW)
            old = old_state[g * (group // NEW) + s]
            from_state = jnp.dot(query[part], old.astype(BF16), preferred_element_type=F32)
            parts.append(from_scale[part] * from_state + in_block[part])
            scales[pl.ds((g * (group // NEW) + s) * 8, 8), :] = last_scale[s * NEW : s * NEW + 8]
        kept = jnp.concatenate(parts, axis=0)
        retained[span, :] = kept
        decayed[span, :] = faded
        values[span, :] = value
        first = jnp.sum(kept, axis=1, keepdims=True)
        second = jnp.sum(kept * kept, axis=1, keepdims=True)
        lanes = lax.broadcasted_iota(jnp.int32, (group, 128), 1)
        stats[span, :] = jnp.where(lanes < 64, first, second)

    def keep(c):
        wide, narrow = pl.ds(c * chunk, chunk), pl.ds(c * (chunk // 4), chunk // 4)
        for i, (src, dst, span) in enumerate(
            ((decayed, decayed_out, wide), (values, value_out, wide), (scales, scale_out, narrow))
        ):
            copy = pltpu.make_async_copy(src.at[span], dst.at[span], out_sems.at[c, i])
            copy.start()
            kept_copies.append(copy)

    def stat_copy(c):
        span = pl.ds(c * chunk, chunk)
        return remote(stats.at[span], other_stats.at[span], stat_sems.at[c, 0], stat_sems.at[c, 1], partner)

    def share_stats(c):
        copy = stat_copy(c)
        copy.start()
        sent.append(copy)

    def gate_copy(c, owner):
        slot = gated.at[owner, pl.ds(c * chunk, chunk)]
        return remote(slot, slot, gate_sems.at[c, 0], gate_sems.at[c, 1], partner)

    def gate(c):
        stat_copy(c).wait_recv()
        tile = min(chunk, 128)

        def body(index, carry):
            span = pl.ds(pl.multiple_of(c * chunk + index * tile, tile), tile)
            both = stats[span, :] + other_stats[span, :]
            centre = both[:, :1] / VHEAD
            variance = both[:, 64:65] / VHEAD - centre * centre
            normed = (retained[span, :] - centre) * lax.rsqrt(variance + EPS)
            g = total[3, span, :]
            gated[core, span, :] = (normed * gain[...] * (g / (1.0 + jnp.exp(-g)))).astype(BF16)
            return carry

        lax.fori_loop(0, chunk // tile, body, 0, unroll=2)
        copy = gate_copy(c, core)
        copy.start()
        sent.append(copy)


    def products(c, j, first, second):
        span = pl.ds(c * chunk, chunk)
        left = jnp.concatenate([gated[0, span, :], gated[1, span, :]], axis=1)
        right = jnp.concatenate(
            [out_rows[place.chip(ORDER[j], first)], out_rows[place.chip(ORDER[j], second)]], axis=1
        )
        return jnp.dot(left, right, preferred_element_type=F32)

    def copy1(c, way, kind, j):
        at = (c, way, kind, j)
        return remote(s1.at[at], r1.at[at], ss1.at[at], rs1.at[at], b_next[way])

    def copy2(c, way, kind):
        at = (c, way, kind)
        return remote(s2.at[at], r2.at[at], ss2.at[at], rs2.at[at], a_next[way])

    def put1(c, way, kind, j, value):
        s1[c, way, kind, j] = value.astype(BF16)
        copy = copy1(c, way, kind, j)
        copy.start()
        sent.append(copy)

    def got1(c, way, kind, j):
        copy1(c, way, kind, j).wait_recv()
        return r1[c, way, kind, j].astype(F32)

    def put2(c, way, kind, value):
        s2[c, way, kind] = value.astype(BF16)
        copy = copy2(c, way, kind)
        copy.start()
        sent.append(copy)

    def got2(c, way, kind):
        copy2(c, way, kind).wait_recv()
        return r2[c, way, kind].astype(F32)

    def far(c, j):
        both = products(c, j, 2, 0)
        put1(c, 0, 0, j, both[:sub, :BLOCK])
        put1(c, 1, 0, j, both[sub:, :BLOCK])
        own1[c, j] = both[:, BLOCK:]

    def plain(c, j):
        both = products(c, j, 1, -1)
        put1(c, 0, 1, j, both[sub:, :BLOCK])
        put1(c, 1, 1, j, both[:sub, BLOCK:])
        near1[c, 0, j] = both[:sub, :BLOCK]
        near1[c, 1, j] = both[sub:, BLOCK:]

    def passing(c, j, way):
        put1(c, way, 2, j, near1[c, way, j] + got1(c, way, 0, j))

    def column(c, j, half):
        return own1[c, j, pl.ds(half * sub, sub), :] + got1(c, half, 2, j) + got1(c, 1 - half, 1, j)

    def row_far(c, way):
        put2(c, way, 0, column(c, 0, way))

    def row_plain(c, way):
        put2(c, way, 1, column(c, 1 + way, 1 - way))

    def row_passing(c, way):
        put2(c, way, 2, column(c, 1 + way, way) + got2(c, way, 0))

    def row_own(c, half):
        own2[rows_of(c, half), :] = column(c, 3, half)

    def finish(c, half):
        span = rows_of(c, half)
        layer_out[span, :] = (own2[span, :] + got2(c, half, 2) + got2(c, 1 - half, 1)).astype(BF16)


    mine = pl.ds(pl.multiple_of(core * BLOCK, BLOCK), BLOCK)
    own_rows = pl.ds(pl.multiple_of(core * 256, 256), 256)
    other_rows = pl.ds(pl.multiple_of((1 - core) * 256, 256), 256)
    loads = [
        pltpu.make_async_copy(tokens, held.at[me], load_sems.at[0]),
        pltpu.make_async_copy(w_query, weights.at[0, :, mine], load_sems.at[1]),
        pltpu.make_async_copy(w_key, weights.at[1, :, mine], load_sems.at[2]),
        pltpu.make_async_copy(w_value, weights.at[2], load_sems.at[3]),
        pltpu.make_async_copy(w_gate, weights.at[3], load_sems.at[4]),
    ]
    exchanged = [
        remote(w_query, weights.at[0, :, mine], side_sems.at[0], side_sems.at[1], partner),
        remote(w_key, weights.at[1, :, mine], side_sems.at[2], side_sems.at[3], partner),
    ]
    state_load = pltpu.make_async_copy(state, old_state, load_sems.at[5])
    out_loads = []
    out_sent = remote(out_rows.at[:, other_rows], out_rows.at[:, other_rows], side_sems.at[4], side_sems.at[5], partner)

    def start_out():
        for chip in range(CHIPS):
            columns = pl.ds(pl.multiple_of(chip * 2 * BLOCK + core * BLOCK, BLOCK), BLOCK)
            load = pltpu.make_async_copy(
                w_out.at[:, columns], out_rows.at[chip, own_rows], load_sems.at[6 + chip]
            )
            load.start()
            out_loads.append(load)
        for chip in range(CHIPS):
            columns = pl.ds(pl.multiple_of(chip * 2 * BLOCK + (1 - core) * BLOCK, BLOCK), BLOCK)
            remote(
                w_out.at[:, columns], out_rows.at[chip, own_rows], side_sems.at[4], side_sems.at[5], partner
            ).start()

    def wait_out():
        for load in out_loads:
            load.wait()
        out_sent.wait()

    ring = a_next + b_next
    own(0, a_next)
    own(0, b_next)
    own(0, (partner,))
    for load in loads:
        load.start()
    for copy in exchanged:
        copy.start()
    state_load.start()
    own(1, a_next)
    own(1, b_next)
    own(1, (partner,))
    decays()
    arrive(0, -1, 0, 0)
    arrive(0, 1, 0, 0)
    arrive(0, 0, -1, 0)
    arrive(0, 0, 1, 0)
    arrive(0, -1, 0, 1)
    arrive(0, 1, 0, 1)
    arrive(0, 0, 1, 1)
    arrive(0, 0, -1, 1)
    for load in loads:
        load.wait()
    for copy in exchanged:
        copy.wait()
    project(0, 0)
    project(1, 0)
    arrive(1, -1, 0, 0)
    arrive(1, 1, 0, 0)
    arrive(1, 0, -1, 0)
    arrive(1, 0, 1, 0)
    project(0, 1)
    project(0, 2)
    start_out()
    arrive(1, -1, 0, 1)
    arrive(1, 1, 0, 1)
    arrive(1, 0, 1, 1)
    arrive(1, 0, -1, 1)
    arrive(0, -1, 1, 0)
    arrive(0, 2, 0, 0)
    arrive(0, -1, -1, 0)
    arrive(0, 2, 0, 1)
    arrive(0, 1, 1, 0)
    arrive(0, 1, -1, 0)
    arrive(0, -1, 1, 1)
    arrive(1, 2, 0, 0)
    arrive(0, 0, 2, 0)
    arrive(0, 1, 1, 1)
    arrive(0, -1, -1, 1)
    arrive(1, 2, 0, 1)
    project(1, 1)
    arrive(0, 0, 2, 1)
    arrive(0, 1, -1, 1)
    project(1, 2)
    wait_out()
    arrive(1, -1, -1, 0)
    arrive(1, -1, 1, 0)
    project(0, 4)
    arrive(1, 1, -1, 0)
    arrive(1, 1, 1, 0)
    project(0, 3)
    arrive(1, -1, 1, 1)
    arrive(1, 0, 2, 0)
    project(0, 5)
    arrive(1, 1, 1, 1)
    arrive(1, -1, -1, 1)
    arrive(1, 0, 2, 1)
    arrive(1, 1, -1, 1)
    project(1, 4)
    arrive(0, 2, -1, 0)
    arrive(0, 2, 1, 0)
    project(1, 3)
    arrive(0, 2, 1, 1)
    arrive(0, -1, 2, 0)
    project(1, 5)
    arrive(0, -1, 2, 1)
    arrive(0, 2, -1, 1)
    arrive(0, 1, 2, 0)
    arrive(1, 2, 1, 0)
    arrive(1, 2, -1, 0)
    arrive(0, 1, 2, 1)
    project(0, 6)
    arrive(1, 2, 1, 1)
    arrive(1, 2, -1, 1)
    project(0, 7)
    arrive(1, -1, 2, 0)
    arrive(1, -1, 2, 1)
    arrive(1, 1, 2, 0)
    arrive(1, 1, 2, 1)
    project(1, 6)
    arrive(0, 2, 2, 0)
    arrive(0, 2, 2, 1)
    project(1, 7)
    arrive(1, 2, 2, 0)
    arrive(1, 2, 2, 1)
    project(0, 8)
    state_load.wait()
    retain(0)
    retain(1)
    share_stats(0)
    project(1, 8)
    retain(2)
    retain(3)
    share_stats(1)
    gate(0)
    keep(0)
    keep(1)
    gate(1)
    gate_copy(0, 1 - core).wait_recv()
    plain(0, 0)
    plain(0, 1)
    plain(0, 2)
    far(0, 0)
    gate_copy(1, 1 - core).wait_recv()
    plain(1, 0)
    plain(1, 1)
    plain(1, 2)
    far(1, 0)
    plain(0, 3)
    plain(1, 3)
    far(0, 1)
    far(1, 1)
    passing(0, 0, 0)
    passing(0, 0, 1)
    far(0, 2)
    far(1, 2)
    far(0, 3)
    far(1, 3)
    passing(1, 0, 0)
    passing(1, 0, 1)
    passing(0, 1, 0)
    passing(0, 1, 1)
    passing(1, 1, 0)
    passing(1, 1, 1)
    row_far(0, 0)
    row_far(0, 1)
    passing(0, 2, 0)
    passing(0, 2, 1)
    passing(1, 2, 0)
    passing(1, 2, 1)
    passing(0, 3, 0)
    passing(0, 3, 1)
    passing(1, 3, 0)
    passing(1, 3, 1)
    row_far(1, 0)
    row_far(1, 1)
    row_passing(0, 0)
    row_plain(0, 0)
    row_plain(1, 0)
    row_passing(0, 1)
    row_plain(0, 1)
    row_passing(1, 0)
    row_passing(1, 1)
    row_plain(1, 1)
    row_own(0, 1)
    row_own(0, 0)
    row_own(1, 1)
    finish(0, 1)
    finish(0, 0)
    row_own(1, 0)
    finish(1, 1)
    finish(1, 0)

    for copy in sent:
        copy.wait_send()
    for copy in kept_copies:
        copy.wait()


def update_kernel(state, decayed, values, scales, new_state, block, keys, held, scale, read_sems, write_sems, in_sems):
    count = state.shape[0]
    step = count // STEPS
    reads, writes = [], []
    inputs = [
        pltpu.make_async_copy(decayed, keys, in_sems.at[0]),
        pltpu.make_async_copy(values, held, in_sems.at[1]),
        pltpu.make_async_copy(scales, scale, in_sems.at[2]),
    ]
    for i in range(STEPS):
        span = pl.ds(i * step, step)
        reads.append(pltpu.make_async_copy(state.at[span], block.at[span], read_sems.at[i]))
        writes.append(pltpu.make_async_copy(block.at[span], new_state.at[span], write_sems.at[i]))
        reads[i].start()
        if i == 0:
            for copy in inputs:
                copy.start()
    for copy in inputs:
        copy.wait()
    for i in range(STEPS):
        reads[i].wait()
        for s in range(i * step, (i + 1) * step):
            part = slice(s * NEW, (s + 1) * NEW)
            fresh = lax.dot_general(keys[part, :], held[part, :], PAIR_TN, preferred_element_type=F32)
            block[s] = scale[s * 8 : s * 8 + 1, :] * block[s] + fresh
        writes[i].start()
    for write in writes:
        write.wait()


def update_state(state, decayed, values, scales):
    outside = pl.BlockSpec(memory_space=pltpu.HBM)
    return pl.pallas_call(
        update_kernel,
        out_shape=jax.ShapeDtypeStruct(state.shape, F32),
        in_specs=[outside] * 4,
        out_specs=outside,
        scratch_shapes=[
            pltpu.VMEM(state.shape, F32),
            pltpu.VMEM(decayed.shape, BF16),
            pltpu.VMEM(values.shape, BF16),
            pltpu.VMEM(scales.shape, F32),
            pltpu.SemaphoreType.DMA((STEPS,)),
            pltpu.SemaphoreType.DMA((STEPS,)),
            pltpu.SemaphoreType.DMA((3,)),
        ],
        compiler_params=pltpu.CompilerParams(vmem_limit_bytes=VMEM_LIMIT),
        name="update_state",
    )(state, decayed, values, scales)


def per_device(tokens, decay, state, w_query, w_key, w_value, w_gate, w_out, norm_gain):
    rows, features = tokens.shape[0], w_query.shape[0]
    chunk = rows // CHUNKS
    sub = chunk // 2
    group = min(GROUP, chunk)
    outside = pl.BlockSpec(memory_space=pltpu.HBM)
    inside = pl.BlockSpec(memory_space=pltpu.VMEM)
    layer_out, decayed, values, scales = pl.pallas_call(
        kernel,
        out_shape=(
            jax.ShapeDtypeStruct((rows, BLOCK), BF16),
            jax.ShapeDtypeStruct((rows, 256), BF16),
            jax.ShapeDtypeStruct((rows, 256), BF16),
            jax.ShapeDtypeStruct((rows // 4, 256), F32),
        ),
        in_specs=[outside, inside, inside] + [outside] * 6,
        out_specs=(inside, outside, outside, outside),
        scratch_shapes=[
            pltpu.VMEM((2 * CHIPS, rows, BLOCK), BF16),
            pltpu.VMEM(state.shape, F32),
            pltpu.VMEM((rows, 256), BF16),
            pltpu.VMEM((rows, 256), BF16),
            pltpu.VMEM((rows // 4, 256), F32),
            pltpu.VMEM((4, features, 256), BF16),
            pltpu.VMEM((4, rows, 256), F32),
            pltpu.VMEM((CHIPS, 512, BLOCK), BF16),
            pltpu.VMEM((rows, 128), F32),
            pltpu.VMEM((rows, 128), F32),
            pltpu.VMEM((rows // group, 8, group), F32),
            pltpu.VMEM((rows, 256), F32),
            pltpu.VMEM((rows, 128), F32),
            pltpu.VMEM((rows, 128), F32),
            pltpu.VMEM((2, rows, 256), BF16),
            pltpu.VMEM((CHUNKS, 4, chunk, BLOCK), F32),
            pltpu.VMEM((CHUNKS, 2, 4, sub, BLOCK), F32),
            pltpu.VMEM((CHUNKS, 2, 3, 4, sub, BLOCK), BF16),
            pltpu.VMEM((CHUNKS, 2, 3, 4, sub, BLOCK), BF16),
            pltpu.VMEM((CHUNKS, 2, 3, sub, BLOCK), BF16),
            pltpu.VMEM((CHUNKS, 2, 3, sub, BLOCK), BF16),
            pltpu.VMEM((rows, BLOCK), F32),
            pltpu.SemaphoreType.DMA((CHUNKS * 64,)),
            pltpu.SemaphoreType.DMA((CHUNKS, 2 * CHIPS, 2)),
            pltpu.SemaphoreType.DMA((6,)),
            pltpu.SemaphoreType.DMA((6 + CHIPS,)),
            pltpu.SemaphoreType.DMA((CHUNKS, 2)),
            pltpu.SemaphoreType.DMA((CHUNKS, 2)),
            pltpu.SemaphoreType.DMA((CHUNKS, 2, 3, 4)),
            pltpu.SemaphoreType.DMA((CHUNKS, 2, 3, 4)),
            pltpu.SemaphoreType.DMA((CHUNKS, 2, 3)),
            pltpu.SemaphoreType.DMA((CHUNKS, 2, 3)),
            pltpu.SemaphoreType.DMA((CHUNKS, 3)),
        ],
        compiler_params=pltpu.CompilerParams(
            collective_id=0, has_side_effects=True, vmem_limit_bytes=VMEM_LIMIT
        ),
        name="retention_step",
    )(tokens, decay.T, norm_gain.reshape(1, -1), state, w_query, w_key, w_value, w_gate, w_out)
    return layer_out, update_state(state, decayed, values, scales)


def solution(mesh):
    placed = (
        P("dp", "mp"),
        P("dp", None),
        P("dp", None, "mp"),
        P(None, "mp"),
        P(None, "mp"),
        P(None, "mp"),
        P(None, "mp"),
        P("mp", None),
        P("mp"),
    )
    return jax.shard_map(
        per_device,
        mesh=mesh,
        in_specs=placed,
        out_specs=(P("dp", "mp"), P("dp", None, "mp")),
        check_vma=False,
    )
```

time: 217 us -> 73.6 us (0.34)
  waiting for transfers between devices: 121 us -> 0 us
  Pallas kernels: 0 us -> 72.1 us
  matrix products: 44.5 us -> 0 us
  local copies, waits for them, and re-layouts: 26.4 us -> 0.71 us
  between operations: 14.3 us -> 0.66 us
  starting transfers between devices: 7.03 us -> 0 us
    all_gather x2 -> x0, waiting for transfers between devices: 91.8 us -> none  [the longest x1 59.4 us: per_device(): segment = lax.all_gather(tokens, 'mp', axis=1, tiled=True)]
    pallas_call x0 -> x2, Pallas kernels: none -> 72.1 us  [the longest x1 64.9 us: per_device(): pl.pallas_call(kernel, out_shape=(jax.ShapeDtypeStruct((rows, BLOCK), BF1...]
    dot_general x8 -> x0, matrix products: 44.5 us -> none  [the longest x4 18.2 us: per_device(): jnp.dot(segment, weight_rows, preferred_element_type=jnp.float32)]
    all_to_all x1 -> x0, waiting for transfers between devices: 27.6 us -> none  [per_device(): lax.all_to_all(w_out, 'mp', split_axis=1, concat_axis=0, tiled=True)]
    unnamed x29 -> x3, local copies, waits for them, and re-layouts: 21.5 us -> 0.71 us
    all_to_all x1 -> x0, starting transfers between devices: 5.76 us -> none  [per_device(): lax.all_to_all(w_out, 'mp', split_axis=1, concat_axis=0, tiled=True)]
    all_to_all x1 -> x0, local copies, waits for them, and re-layouts: 2.92 us -> none  [per_device(): lax.all_to_all(w_out, 'mp', split_axis=1, concat_axis=0, tiled=True)]
  transfers between devices with their start and end apart: 7 -> 0, of which waited for: 5 -> 0; matrix products, arithmetic and copies ran while one was open for 19% -> 0% of each run, Pallas kernels for 0% -> 0%
where the time goes in v3:
time: 73.6 us; the launch traced here: 73.5 us
  Pallas kernels  72.1 us (98%)
    pallas_call x1, Pallas kernels, per_device(): pl.pallas_call(kernel, out_shape=(jax.ShapeDtypeStruct((rows, BLOCK), BF1...  64.9 us
    pallas_call x1, Pallas kernels, update_state(): pl.pallas_call(update_kernel, out_shape=jax.ShapeDtypeStruct(state.shape,...  7.25 us

profile of v3, /device:TPU:0, one launch (start us, length us, event | category | flops | bytes accessed | tf_op | source)
XLA Modules:
  0.0 73.5 jit_solution(14068871161456470964)
XLA Ops:
  0.6 64.9 %retention_step.1 = (bf16[1024,128]{1,0:T(8,128)(2,1)}, bf16[1024,256]{1,0:T(8,128)(2,1)}, bf16[1024,256]{1,0:T(8,128)(2,1)}, f32[256,256]{1,0:T(8,128)}) custom-call(bf16[1024,128]{1,0:T(8,128)(2,1)} %tokens.1, f32[16,1024]{1,0:T(8,128)} %bitcast.2, f32[1,256]{1,0:T(1,128)} %bitcast.3, f32[32,256,256]{2,1,0:T(8,128)} %state.3, bf16[4096,128]{1,0:T(8,128)(2,1)} %w_query.1, ...), custom_call_target="tpu_custom_call" | custom-call | tf_op jit(solution)/shard_map/retention_step/pallas_call | solution.py:630
  65.5 0.0 copy-start
  65.5 7.3 %update_state.1 = f32[32,256,256]{2,1,0:T(8,128)} custom-call(f32[32,256,256]{2,1,0:T(8,128)} %state.3, bf16[1024,256]{1,0:T(8,128)(2,1)} %get-tuple-element.7.decayed, bf16[1024,256]{1,0:T(8,128)(2,1)} %get-tuple-element.8.values, f32[256,256]{1,0:T(8,128)} %get-tuple-element.9.scales), custom_call_target="tpu_custom_call" | custom-call | tf_op jit(solution)/shard_map/update_state/pallas_call | solution.py:604
  72.8 0.0 copy-done
  72.8 0.7 copy.12
Async XLA Ops:
  65.5 7.3 %copy-start = (bf16[1024,128]{1,0:T(8,128)(2,1)S(1)}, bf16[1024,128]{1,0:T(8,128)(2,1)}, u32[]{:S(2)}) copy-start(bf16[1024,128]{1,0:T(8,128)(2,1)} %get-tuple-element.12) | copy-start | bytes 786436

commit v4 on v3

--- a/solution.py
+++ b/solution.py
@@ -12,8 +12,8 @@
 NEW = 32
 EPS = 0.1
 CHUNKS = 2
-STEPS = 8
-VMEM_LIMIT = 62 * 2**20
+STEPS = 4
+VMEM_LIMIT = 46 * 2**20
 SIDE = 4
 CHIPS = SIDE * SIDE
 BLOCK = 128
@@ -69,17 +69,6 @@
     pl.semaphore_wait(barrier, len(others))
 
 
-ARRIVALS = (
-    ((-1, 0, 0), (1, 0, 0), (0, -1, 0), (0, 1, 0)),
-    ((-1, 0, 1), (1, 0, 1)),
-    ((0, -1, 1), (0, 1, 1)),
-    ((-1, -1, 0), (-1, 1, 0), (1, -1, 0), (1, 1, 0), (2, 0, 0), (2, 0, 1), (0, 2, 0), (0, 2, 1)),
-    ((-1, -1, 1), (-1, 1, 1)),
-    ((1, -1, 1), (1, 1, 1)),
-    ((2, -1, 0), (2, 1, 0), (2, -1, 1), (2, 1, 1)),
-    ((-1, 2, 0), (-1, 2, 1), (1, 2, 0), (1, 2, 1)),
-    ((2, 2, 0), (2, 2, 1)),
-)
 PAIRS = {
     1: ((-1, 0), (1, 0)),
     2: ((0, -1), (0, 1)),
@@ -89,6 +78,12 @@
     6: ((2, -1), (2, 1)),
     7: ((-1, 2), (1, 2)),
 }
+STEP_OF = {(0, 0): 0, (2, 2): 8} | {block: step for step, pair in PAIRS.items() for block in pair}
+SEEN = [block + (half,) for block in STEP_OF if block != (0, 0) for half in range(2)]
+
+
+def wrap(distance):
+    return (distance + 1) % SIDE - 1
 
 
 ORDER = (2, 1, -1, 0)
@@ -98,11 +93,12 @@
 
 
 def kernel(
-    tokens, decay, gain, state, w_query, w_key, w_value, w_gate, w_out,
-    layer_out, decayed_out, value_out, scale_out,
-    held, old_state, decayed, values, scales, weights, total, out_rows, cumul, final, along,
+    tokens, decay_in, gain_in, state, w_query, w_key, w_value, w_gate, w_out,
+    layer_out, new_state,
+    held, decay, gain, weights, total, out_rows, cumul, final, along,
     retained, stats, other_stats, gated, own1, near1, s1, r1, s2, r2, own2,
-    send_sems, recv_sems, side_sems, load_sems, stat_sems, gate_sems, ss1, rs1, ss2, rs2, out_sems,
+    send_sems, recv_sems, pair_sems, side_sems, load_sems, stat_sems, gate_sems,
+    far1_sems, near1_sems, far2_sems, near2_sems,
 ):
     place = Place()
     rows = tokens.shape[0]
@@ -112,8 +108,6 @@
     me, core, partner = place.me, place.core, place.partner
     a_next = (place.at(1, 0), place.at(-1, 0))
     b_next = (place.at(0, 1), place.at(0, -1))
-    sent, kept_copies = [], []
-    counts = [0]
 
     greet(place)
 
@@ -121,44 +115,39 @@
     def rows_of(c, half):
         return pl.ds(c * chunk + half * sub, sub)
 
-    def send(src, block, c, half, device):
-        copy = remote(
-            src, held.at[block, rows_of(c, half)],
-            send_sems.at[counts[0]], recv_sems.at[c, block, half], device,
-        )
-        counts[0] += 1
-        copy.start()
-        sent.append(copy)
-
-    def own(c, devices):
+    def send(src, block, c, half, way, da, db):
+        if way == "d":
+            device, sem = partner, pair_sems.at[c, STEP_OF[da, db]]
+        else:
+            step = 1 if way[1] == "+" else -1
+            device = place.at(*((step, 0) if way[0] == "a" else (0, step)))
+            seen = (wrap(da - step), db) if way[0] == "a" else (da, wrap(db - step))
+            sem = recv_sems.at[c, SEEN.index(seen + (half,))]
+        remote(src, held.at[block, rows_of(c, half)], send_sems.at[0], sem, device).start()
+
+    def own(c, ways):
         for half in range(2):
-            for device in devices:
-                send(tokens.at[rows_of(c, half)], me, c, half, device)
-
-    def wait_for(block, c, half):
-        slot = held.at[block, rows_of(c, half)]
-        remote(slot, slot, send_sems.at[0], recv_sems.at[c, block, half], partner).wait_recv()
+            for way in ways:
+                send(tokens.at[rows_of(c, half)], me, c, half, way, 0, 0)
 
     def arrive(c, da, db, half):
         block = place.at(da, db)
-        wait_for(block, c, half)
         slot = held.at[block, rows_of(c, half)]
+        remote(slot, slot, send_sems.at[0], recv_sems.at[c, SEEN.index((da, db, half))], partner).wait_recv()
         if db == 0:
+            ways = ["b+", "b-", "d"]
             if (da, half) == (-1, 0):
-                send(slot, block, c, half, a_next[0])
+                ways.insert(0, "a+")
             if (da, half) == (1, 1):
-                send(slot, block, c, half, a_next[1])
-            send(slot, block, c, half, b_next[0])
-            send(slot, block, c, half, b_next[1])
+                ways.insert(0, "a-")
         elif (db, half) == (-1, 0):
-            send(slot, block, c, half, b_next[0])
+            ways = ["b+", "d"]
         elif (db, half) == (1, 1):
-            send(slot, block, c, half, b_next[1])
-        send(slot, block, c, half, partner)
-
-    def arrivals(c, stage):
-        for event in ARRIVALS[stage]:
-            arrive(c, *event)
+            ways = ["b-", "d"]
+        else:
+            ways = ["d"]
+        for way in ways:
+            send(slot, block, c, half, way, da, db)
 
     def project(c, step):
         if step == 0:
@@ -169,9 +158,8 @@
         else:
             theirs = [place.partner_at(2, 2)]
             blocks = [place.at(2, 2)] + theirs
-        for block in theirs:
-            for half in range(2):
-                wait_for(block, c, half)
+        slots = held.at[pl.ds(0, len(theirs)), pl.ds(c * chunk, chunk)]
+        remote(slots, slots, send_sems.at[0], pair_sems.at[c, step], partner).wait_recv()
         starts = [pl.multiple_of(block * BLOCK, BLOCK) for block in blocks]
         span = pl.ds(c * chunk, chunk)
 
@@ -236,40 +224,28 @@
         parts = []
         for s in range(group // NEW):
             part = slice(s * NEW, (s + 1) * NEW)
-            old = old_state[g * (group // NEW) + s]
+            old = new_state[g * (group // NEW) + s]
             from_state = jnp.dot(query[part], old.astype(BF16), preferred_element_type=F32)
             parts.append(from_scale[part] * from_state + in_block[part])
-            scales[pl.ds((g * (group // NEW) + s) * 8, 8), :] = last_scale[s * NEW : s * NEW + 8]
+            fresh = lax.dot_general(faded[part], value[part], PAIR_TN, preferred_element_type=F32)
+            new_state[g * (group // NEW) + s] = last_scale[s * NEW : s * NEW + 1] * old + fresh
         kept = jnp.concatenate(parts, axis=0)
         retained[span, :] = kept
-        decayed[span, :] = faded
-        values[span, :] = value
         first = jnp.sum(kept, axis=1, keepdims=True)
         second = jnp.sum(kept * kept, axis=1, keepdims=True)
         lanes = lax.broadcasted_iota(jnp.int32, (group, 128), 1)
         stats[span, :] = jnp.where(lanes < 64, first, second)
 
-    def keep(c):
-        wide, narrow = pl.ds(c * chunk, chunk), pl.ds(c * (chunk // 4), chunk // 4)
-        for i, (src, dst, span) in enumerate(
-            ((decayed, decayed_out, wide), (values, value_out, wide), (scales, scale_out, narrow))
-        ):
-            copy = pltpu.make_async_copy(src.at[span], dst.at[span], out_sems.at[c, i])
-            copy.start()
-            kept_copies.append(copy)
-
     def stat_copy(c):
         span = pl.ds(c * chunk, chunk)
-        return remote(stats.at[span], other_stats.at[span], stat_sems.at[c, 0], stat_sems.at[c, 1], partner)
+        return remote(stats.at[span], other_stats.at[span], send_sems.at[3], stat_sems.at[c], partner)
 
     def share_stats(c):
-        copy = stat_copy(c)
-        copy.start()
-        sent.append(copy)
+        stat_copy(c).start()
 
     def gate_copy(c, owner):
         slot = gated.at[owner, pl.ds(c * chunk, chunk)]
-        return remote(slot, slot, gate_sems.at[c, 0], gate_sems.at[c, 1], partner)
+        return remote(slot, slot, send_sems.at[4], gate_sems.at[c], partner)
 
     def gate(c):
         stat_copy(c).wait_recv()
@@ -286,9 +262,7 @@
             return carry
 
         lax.fori_loop(0, chunk // tile, body, 0, unroll=2)
-        copy = gate_copy(c, core)
-        copy.start()
-        sent.append(copy)
+        gate_copy(c, core).start()
 
 
     def products(c, j, first, second):
@@ -299,33 +273,20 @@
         )
         return jnp.dot(left, right, preferred_element_type=F32)
 
-    def copy1(c, way, kind, j):
+    def put1(c, way, kind, j, value):
         at = (c, way, kind, j)
-        return remote(s1.at[at], r1.at[at], ss1.at[at], rs1.at[at], b_next[way])
-
-    def copy2(c, way, kind):
+        s1[at] = value.astype(BF16)
+        sem = far1_sems.at[c, way, j] if kind == 0 else near1_sems.at[c, j, way if kind == 2 else 1 - way]
+        remote(s1.at[at], r1.at[at], send_sems.at[1], sem, b_next[way]).start()
+
+    def put2(c, way, kind, value):
         at = (c, way, kind)
-        return remote(s2.at[at], r2.at[at], ss2.at[at], rs2.at[at], a_next[way])
-
-    def put1(c, way, kind, j, value):
-        s1[c, way, kind, j] = value.astype(BF16)
-        copy = copy1(c, way, kind, j)
-        copy.start()
-        sent.append(copy)
-
-    def got1(c, way, kind, j):
-        copy1(c, way, kind, j).wait_recv()
-        return r1[c, way, kind, j].astype(F32)
-
-    def put2(c, way, kind, value):
-        s2[c, way, kind] = value.astype(BF16)
-        copy = copy2(c, way, kind)
-        copy.start()
-        sent.append(copy)
-
-    def got2(c, way, kind):
-        copy2(c, way, kind).wait_recv()
-        return r2[c, way, kind].astype(F32)
+        s2[at] = value.astype(BF16)
+        sem = far2_sems.at[c, way] if kind == 0 else near2_sems.at[c, way if kind == 2 else 1 - way]
+        remote(s2.at[at], r2.at[at], send_sems.at[2], sem, a_next[way]).start()
+
+    def await_into(slot, sem):
+        remote(slot, slot, send_sems.at[0], sem, partner).wait_recv()
 
     def far(c, j):
         both = products(c, j, 2, 0)
@@ -341,26 +302,42 @@
         near1[c, 1, j] = both[sub:, BLOCK:]
 
     def passing(c, j, way):
-        put1(c, way, 2, j, near1[c, way, j] + got1(c, way, 0, j))
+        await_into(r1.at[c, way, 0, j], far1_sems.at[c, way, j])
+        put1(c, way, 2, j, near1[c, way, j] + r1[c, way, 0, j].astype(F32))
 
     def column(c, j, half):
-        return own1[c, j, pl.ds(half * sub, sub), :] + got1(c, half, 2, j) + got1(c, 1 - half, 1, j)
+        return (
+            own1[c, j, pl.ds(half * sub, sub), :]
+            + r1[c, half, 2, j].astype(F32)
+            + r1[c, 1 - half, 1, j].astype(F32)
+        )
+
+    def await_column(c, j, half):
+        await_into(r1.at[c, :, 1, j], near1_sems.at[c, j, half])
 
     def row_far(c, way):
+        await_column(c, 0, way)
         put2(c, way, 0, column(c, 0, way))
 
     def row_plain(c, way):
+        await_column(c, 1 + way, 1 - way)
         put2(c, way, 1, column(c, 1 + way, 1 - way))
 
     def row_passing(c, way):
-        put2(c, way, 2, column(c, 1 + way, way) + got2(c, way, 0))
+        await_column(c, 1 + way, way)
+        await_into(r2.at[c, way, 0], far2_sems.at[c, way])
+        put2(c, way, 2, column(c, 1 + way, way) + r2[c, way, 0].astype(F32))
 
     def row_own(c, half):
+        await_column(c, 3, half)
         own2[rows_of(c, half), :] = column(c, 3, half)
 
     def finish(c, half):
         span = rows_of(c, half)
-        layer_out[span, :] = (own2[span, :] + got2(c, half, 2) + got2(c, 1 - half, 1)).astype(BF16)
+        await_into(r2.at[c, :, 1], near2_sems.at[c, half])
+        layer_out[span, :] = (
+            own2[span, :] + r2[c, half, 2].astype(F32) + r2[c, 1 - half, 1].astype(F32)
+        ).astype(BF16)
 
 
     mine = pl.ds(pl.multiple_of(core * BLOCK, BLOCK), BLOCK)
@@ -377,18 +354,17 @@
         remote(w_query, weights.at[0, :, mine], side_sems.at[0], side_sems.at[1], partner),
         remote(w_key, weights.at[1, :, mine], side_sems.at[2], side_sems.at[3], partner),
     ]
-    state_load = pltpu.make_async_copy(state, old_state, load_sems.at[5])
-    out_loads = []
+    small_loads = [
+        pltpu.make_async_copy(decay_in, decay, load_sems.at[7]),
+        pltpu.make_async_copy(gain_in, gain, load_sems.at[8]),
+    ]
+    state_load = pltpu.make_async_copy(state, new_state, load_sems.at[5])
     out_sent = remote(out_rows.at[:, other_rows], out_rows.at[:, other_rows], side_sems.at[4], side_sems.at[5], partner)
 
     def start_out():
         for chip in range(CHIPS):
             columns = pl.ds(pl.multiple_of(chip * 2 * BLOCK + core * BLOCK, BLOCK), BLOCK)
-            load = pltpu.make_async_copy(
-                w_out.at[:, columns], out_rows.at[chip, own_rows], load_sems.at[6 + chip]
-            )
-            load.start()
-            out_loads.append(load)
+            pltpu.make_async_copy(w_out.at[:, columns], out_rows.at[chip, own_rows], load_sems.at[6]).start()
         for chip in range(CHIPS):
             columns = pl.ds(pl.multiple_of(chip * 2 * BLOCK + (1 - core) * BLOCK, BLOCK), BLOCK)
             remote(
@@ -396,22 +372,23 @@
             ).start()
 
     def wait_out():
-        for load in out_loads:
-            load.wait()
+        slots = out_rows.at[:, own_rows]
+        pltpu.make_async_copy(slots, slots, load_sems.at[6]).wait()
         out_sent.wait()
 
-    ring = a_next + b_next
-    own(0, a_next)
-    own(0, b_next)
-    own(0, (partner,))
-    for load in loads:
+    own(0, ("a+", "a-"))
+    own(0, ("b+", "b-"))
+    own(0, ("d",))
+    for load in small_loads + loads:
         load.start()
     for copy in exchanged:
         copy.start()
     state_load.start()
-    own(1, a_next)
-    own(1, b_next)
-    own(1, (partner,))
+    own(1, ("a+", "a-"))
+    own(1, ("b+", "b-"))
+    own(1, ("d",))
+    for load in small_loads:
+        load.wait()
     decays()
     arrive(0, -1, 0, 0)
     arrive(0, 1, 0, 0)
@@ -505,8 +482,6 @@
     retain(3)
     share_stats(1)
     gate(0)
-    keep(0)
-    keep(1)
     gate(1)
     gate_copy(0, 1 - core).wait_recv()
     plain(0, 0)
@@ -563,61 +538,32 @@
     finish(1, 1)
     finish(1, 0)
 
-    for copy in sent:
-        copy.wait_send()
-    for copy in kept_copies:
-        copy.wait()
-
-
-def update_kernel(state, decayed, values, scales, new_state, block, keys, held, scale, read_sems, write_sems, in_sems):
-    count = state.shape[0]
-    step = count // STEPS
-    reads, writes = [], []
-    inputs = [
-        pltpu.make_async_copy(decayed, keys, in_sems.at[0]),
-        pltpu.make_async_copy(values, held, in_sems.at[1]),
-        pltpu.make_async_copy(scales, scale, in_sems.at[2]),
-    ]
+    for sem, slots in enumerate((held.at[pl.ds(0, 2 * CHIPS - 1)], s1, s2, stats, gated.at[core])):
+        remote(slots, slots, send_sems.at[sem], stat_sems.at[0], partner).wait_send()
+
+
+def store_kernel(out_in, state_in, out, state, sems):
+    step = state.shape[0] // STEPS
+    copies = [pltpu.make_async_copy(out_in, out, sems.at[STEPS])]
     for i in range(STEPS):
         span = pl.ds(i * step, step)
-        reads.append(pltpu.make_async_copy(state.at[span], block.at[span], read_sems.at[i]))
-        writes.append(pltpu.make_async_copy(block.at[span], new_state.at[span], write_sems.at[i]))
-        reads[i].start()
-        if i == 0:
-            for copy in inputs:
-                copy.start()
-    for copy in inputs:
+        copies.append(pltpu.make_async_copy(state_in.at[span], state.at[span], sems.at[i]))
+    for copy in copies:
+        copy.start()
+    for copy in copies:
         copy.wait()
-    for i in range(STEPS):
-        reads[i].wait()
-        for s in range(i * step, (i + 1) * step):
-            part = slice(s * NEW, (s + 1) * NEW)
-            fresh = lax.dot_general(keys[part, :], held[part, :], PAIR_TN, preferred_element_type=F32)
-            block[s] = scale[s * 8 : s * 8 + 1, :] * block[s] + fresh
-        writes[i].start()
-    for write in writes:
-        write.wait()
-
-
-def update_state(state, decayed, values, scales):
-    outside = pl.BlockSpec(memory_space=pltpu.HBM)
+
+
+def store(out, state):
     return pl.pallas_call(
-        update_kernel,
-        out_shape=jax.ShapeDtypeStruct(state.shape, F32),
-        in_specs=[outside] * 4,
-        out_specs=outside,
-        scratch_shapes=[
-            pltpu.VMEM(state.shape, F32),
-            pltpu.VMEM(decayed.shape, BF16),
-            pltpu.VMEM(values.shape, BF16),
-            pltpu.VMEM(scales.shape, F32),
-            pltpu.SemaphoreType.DMA((STEPS,)),
-            pltpu.SemaphoreType.DMA((STEPS,)),
-            pltpu.SemaphoreType.DMA((3,)),
-        ],
-        compiler_params=pltpu.CompilerParams(vmem_limit_bytes=VMEM_LIMIT),
-        name="update_state",
-    )(state, decayed, values, scales)
+        store_kernel,
+        out_shape=(jax.ShapeDtypeStruct(out.shape, out.dtype), jax.ShapeDtypeStruct(state.shape, F32)),
+        in_specs=[pl.BlockSpec(memory_space=pltpu.VMEM)] * 2,
+        out_specs=(pl.BlockSpec(memory_space=pltpu.HBM),) * 2,
+        scratch_shapes=[pltpu.SemaphoreType.DMA((STEPS + 1,))],
+        compiler_params=pltpu.CompilerParams(vmem_limit_bytes=2**20),
+        name="store",
+    )(out, state)
 
 
 def per_device(tokens, decay, state, w_query, w_key, w_value, w_gate, w_out, norm_gain):
@@ -627,22 +573,18 @@
     group = min(GROUP, chunk)
     outside = pl.BlockSpec(memory_space=pltpu.HBM)
     inside = pl.BlockSpec(memory_space=pltpu.VMEM)
-    layer_out, decayed, values, scales = pl.pallas_call(
+    layer_out, new_state = pl.pallas_call(
         kernel,
         out_shape=(
-            jax.ShapeDtypeStruct((rows, BLOCK), BF16),
-            jax.ShapeDtypeStruct((rows, 256), BF16),
-            jax.ShapeDtypeStruct((rows, 256), BF16),
-            jax.ShapeDtypeStruct((rows // 4, 256), F32),
+            pltpu.VMEM((rows, BLOCK), BF16),
+            pltpu.VMEM(state.shape, F32),
         ),
-        in_specs=[outside, inside, inside] + [outside] * 6,
-        out_specs=(inside, outside, outside, outside),
+        in_specs=[outside] * 9,
+        out_specs=(inside,) * 2,
         scratch_shapes=[
             pltpu.VMEM((2 * CHIPS, rows, BLOCK), BF16),
-            pltpu.VMEM(state.shape, F32),
-            pltpu.VMEM((rows, 256), BF16),
-            pltpu.VMEM((rows, 256), BF16),
-            pltpu.VMEM((rows // 4, 256), F32),
+            pltpu.VMEM((decay.shape[1], rows), F32),
+            pltpu.VMEM((1, 256), F32),
             pltpu.VMEM((4, features, 256), BF16),
             pltpu.VMEM((4, rows, 256), F32),
             pltpu.VMEM((CHIPS, 512, BLOCK), BF16),
@@ -660,24 +602,24 @@
             pltpu.VMEM((CHUNKS, 2, 3, sub, BLOCK), BF16),
             pltpu.VMEM((CHUNKS, 2, 3, sub, BLOCK), BF16),
             pltpu.VMEM((rows, BLOCK), F32),
-            pltpu.SemaphoreType.DMA((CHUNKS * 64,)),
-            pltpu.SemaphoreType.DMA((CHUNKS, 2 * CHIPS, 2)),
+            pltpu.SemaphoreType.DMA((5,)),
+            pltpu.SemaphoreType.DMA((CHUNKS, len(SEEN))),
+            pltpu.SemaphoreType.DMA((CHUNKS, 9)),
             pltpu.SemaphoreType.DMA((6,)),
-            pltpu.SemaphoreType.DMA((6 + CHIPS,)),
+            pltpu.SemaphoreType.DMA((9,)),
+            pltpu.SemaphoreType.DMA((CHUNKS,)),
+            pltpu.SemaphoreType.DMA((CHUNKS,)),
+            pltpu.SemaphoreType.DMA((CHUNKS, 2, 4)),
+            pltpu.SemaphoreType.DMA((CHUNKS, 4, 2)),
             pltpu.SemaphoreType.DMA((CHUNKS, 2)),
             pltpu.SemaphoreType.DMA((CHUNKS, 2)),
-            pltpu.SemaphoreType.DMA((CHUNKS, 2, 3, 4)),
-            pltpu.SemaphoreType.DMA((CHUNKS, 2, 3, 4)),
-            pltpu.SemaphoreType.DMA((CHUNKS, 2, 3)),
-            pltpu.SemaphoreType.DMA((CHUNKS, 2, 3)),
-            pltpu.SemaphoreType.DMA((CHUNKS, 3)),
         ],
         compiler_params=pltpu.CompilerParams(
             collective_id=0, has_side_effects=True, vmem_limit_bytes=VMEM_LIMIT
         ),
         name="retention_step",
     )(tokens, decay.T, norm_gain.reshape(1, -1), state, w_query, w_key, w_value, w_gate, w_out)
-    return layer_out, update_state(state, decayed, values, scales)
+    return store(layer_out, new_state)
 
 
 def solution(mesh):

time: 73.6 us -> 64.7 us (0.88)
  Pallas kernels: 72.1 us -> 63.8 us
    pallas_call x2, Pallas kernels: 72.1 us -> 63.8 us  [the longest x1 60.4 us: per_device(): pl.pallas_call(kernel, out_shape=(pltpu.VMEM((rows, BLOCK), BF16), pltpu....]
where the time goes in v4:
time: 64.7 us; the launch traced here: 64.6 us
  Pallas kernels  63.8 us (99%)
  between operations  0.8 us (1%)
    pallas_call x1, Pallas kernels, per_device(): pl.pallas_call(kernel, out_shape=(pltpu.VMEM((rows, BLOCK), BF16), pltpu....  60.4 us
    pallas_call x1, Pallas kernels, store(): pl.pallas_call(store_kernel, out_shape=(jax.ShapeDtypeStruct(out.shape, o...  3.46 us

profile of v4, /device:TPU:0, one launch (start us, length us, event | category | flops | bytes accessed | tf_op | source)
XLA Modules:
  0.0 64.6 jit_solution(8775264023001002531)
XLA Ops:
  0.6 60.4 %retention_step.1 = (bf16[1024,128]{1,0:T(8,128)(2,1)S(1)}, f32[32,256,256]{2,1,0:T(8,128)S(1)}) custom-call(bf16[1024,128]{1,0:T(8,128)(2,1)} %tokens.1, f32[16,1024]{1,0:T(8,128)} %bitcast.2, f32[1,256]{1,0:T(1,128)} %bitcast.3, f32[32,256,256]{2,1,0:T(8,128)} %state.1, bf16[4096,128]{1,0:T(8,128)(2,1)} %w_query.1, bf16[4096,128]{1,0:T(8,128)(2,1)} %w_key.1, ...), custom_call_target="tpu_custom_call" | custom-call | tf_op jit(solution)/shard_map/retention_step/pallas_call | solution.py:576
  61.0 3.5 %store.1 = (bf16[1024,128]{1,0:T(8,128)(2,1)}, f32[32,256,256]{2,1,0:T(8,128)}) custom-call(bf16[1024,128]{1,0:T(8,128)(2,1)S(1)} %get-tuple-element.4.out_in, f32[32,256,256]{2,1,0:T(8,128)S(1)} %get-tuple-element.5.state_in), custom_call_target="tpu_custom_call" | custom-call | tf_op jit(solution)/shard_map/store/pallas_call | solution.py:558

commit v5 on v4

--- a/solution.py
+++ b/solution.py
@@ -66,7 +66,10 @@
     others = (place.partner, place.at(1, 0), place.at(-1, 0), place.at(0, 1), place.at(0, -1))
     for other in others:
         pl.semaphore_signal(barrier, inc=1, device_id={"mp": other}, device_id_type=MESH)
-    pl.semaphore_wait(barrier, len(others))
+
+
+def meet():
+    pl.semaphore_wait(pltpu.get_barrier_semaphore(), 5)
 
 
 PAIRS = {
@@ -128,7 +131,7 @@
     def own(c, ways):
         for half in range(2):
             for way in ways:
-                send(tokens.at[rows_of(c, half)], me, c, half, way, 0, 0)
+                send(held.at[me, rows_of(c, half)], me, c, half, way, 0, 0)
 
     def arrive(c, da, db, half):
         block = place.at(da, db)
@@ -344,7 +347,6 @@
     own_rows = pl.ds(pl.multiple_of(core * 256, 256), 256)
     other_rows = pl.ds(pl.multiple_of((1 - core) * 256, 256), 256)
     loads = [
-        pltpu.make_async_copy(tokens, held.at[me], load_sems.at[0]),
         pltpu.make_async_copy(w_query, weights.at[0, :, mine], load_sems.at[1]),
         pltpu.make_async_copy(w_key, weights.at[1, :, mine], load_sems.at[2]),
         pltpu.make_async_copy(w_value, weights.at[2], load_sems.at[3]),
@@ -354,6 +356,7 @@
         remote(w_query, weights.at[0, :, mine], side_sems.at[0], side_sems.at[1], partner),
         remote(w_key, weights.at[1, :, mine], side_sems.at[2], side_sems.at[3], partner),
     ]
+    token_load = pltpu.make_async_copy(tokens, held.at[me], load_sems.at[0])
     small_loads = [
         pltpu.make_async_copy(decay_in, decay, load_sems.at[7]),
         pltpu.make_async_copy(gain_in, gain, load_sems.at[8]),
@@ -376,17 +379,16 @@
         pltpu.make_async_copy(slots, slots, load_sems.at[6]).wait()
         out_sent.wait()
 
+    for load in [token_load] + small_loads + loads:
+        load.start()
+    state_load.start()
+    token_load.wait()
+    meet()
     own(0, ("a+", "a-"))
     own(0, ("b+", "b-"))
     own(0, ("d",))
-    for load in small_loads + loads:
-        load.start()
     for copy in exchanged:
         copy.start()
-    state_load.start()
-    own(1, ("a+", "a-"))
-    own(1, ("b+", "b-"))
-    own(1, ("d",))
     for load in small_loads:
         load.wait()
     decays()
@@ -398,145 +400,148 @@
     arrive(0, 1, 0, 1)
     arrive(0, 0, 1, 1)
     arrive(0, 0, -1, 1)
+    own(1, ("d",))
+    arrive(0, -1, 1, 0)
     for load in loads:
         load.wait()
     for copy in exchanged:
         copy.wait()
+    start_out()
     project(0, 0)
+    arrive(0, 2, 0, 0)
+    arrive(0, -1, -1, 0)
+    arrive(0, 1, 1, 0)
     project(1, 0)
+    arrive(0, 1, -1, 0)
+    project(0, 1)
+    arrive(0, 2, 0, 1)
+    arrive(0, -1, 1, 1)
+    arrive(0, 0, 2, 0)
+    project(0, 2)
+    arrive(0, 1, 1, 1)
+    arrive(0, -1, -1, 1)
+    arrive(0, 0, 2, 1)
+    own(1, ("a+", "a-"))
+    arrive(0, 1, -1, 1)
+    arrive(0, 2, -1, 0)
+    arrive(0, 2, 1, 0)
+    project(0, 4)
+    arrive(0, 2, 1, 1)
+    arrive(0, -1, 2, 0)
+    wait_out()
+    own(1, ("b+", "b-"))
+    project(0, 3)
+    project(0, 5)
+    arrive(0, -1, 2, 1)
+    arrive(0, 1, 2, 0)
     arrive(1, -1, 0, 0)
     arrive(1, 1, 0, 0)
+    arrive(0, 1, 2, 1)
+    arrive(0, 2, -1, 1)
+    arrive(1, -1, 0, 1)
+    arrive(1, 1, 0, 1)
+    arrive(0, 2, 2, 0)
+    arrive(0, 2, 2, 1)
+    project(0, 7)
+    project(0, 6)
     arrive(1, 0, -1, 0)
     arrive(1, 0, 1, 0)
-    project(0, 1)
-    project(0, 2)
-    start_out()
-    arrive(1, -1, 0, 1)
-    arrive(1, 1, 0, 1)
+    project(1, 1)
+    arrive(1, 2, 0, 0)
     arrive(1, 0, 1, 1)
+    project(0, 8)
     arrive(1, 0, -1, 1)
-    arrive(0, -1, 1, 0)
-    arrive(0, 2, 0, 0)
-    arrive(0, -1, -1, 0)
-    arrive(0, 2, 0, 1)
-    arrive(0, 1, 1, 0)
-    arrive(0, 1, -1, 0)
-    arrive(0, -1, 1, 1)
-    arrive(1, 2, 0, 0)
-    arrive(0, 0, 2, 0)
-    arrive(0, 1, 1, 1)
-    arrive(0, -1, -1, 1)
-    arrive(1, 2, 0, 1)
-    project(1, 1)
-    arrive(0, 0, 2, 1)
-    arrive(0, 1, -1, 1)
-    project(1, 2)
-    wait_out()
+    state_load.wait()
+    retain(0)
     arrive(1, -1, -1, 0)
     arrive(1, -1, 1, 0)
-    project(0, 4)
+    arrive(1, 2, 0, 1)
+    retain(1)
     arrive(1, 1, -1, 0)
     arrive(1, 1, 1, 0)
-    project(0, 3)
+    share_stats(0)
+    project(1, 2)
     arrive(1, -1, 1, 1)
+    arrive(1, -1, -1, 1)
+    arrive(1, 1, 1, 1)
+    arrive(1, 1, -1, 1)
+    gate(0)
     arrive(1, 0, 2, 0)
-    project(0, 5)
-    arrive(1, 1, 1, 1)
-    arrive(1, -1, -1, 1)
+    arrive(1, 2, 1, 0)
+    project(1, 4)
+    arrive(1, 2, -1, 0)
     arrive(1, 0, 2, 1)
-    arrive(1, 1, -1, 1)
-    project(1, 4)
-    arrive(0, 2, -1, 0)
-    arrive(0, 2, 1, 0)
-    project(1, 3)
-    arrive(0, 2, 1, 1)
-    arrive(0, -1, 2, 0)
     project(1, 5)
-    arrive(0, -1, 2, 1)
-    arrive(0, 2, -1, 1)
-    arrive(0, 1, 2, 0)
-    arrive(1, 2, 1, 0)
-    arrive(1, 2, -1, 0)
-    arrive(0, 1, 2, 1)
-    project(0, 6)
     arrive(1, 2, 1, 1)
+    arrive(1, -1, 2, 0)
+    gate_copy(0, 1 - core).wait_recv()
+    far(0, 0)
+    arrive(1, -1, 2, 1)
     arrive(1, 2, -1, 1)
-    project(0, 7)
-    arrive(1, -1, 2, 0)
-    arrive(1, -1, 2, 1)
+    far(0, 1)
+    far(0, 2)
     arrive(1, 1, 2, 0)
     arrive(1, 1, 2, 1)
+    far(0, 3)
+    arrive(1, 2, 2, 0)
+    plain(0, 0)
+    arrive(1, 2, 2, 1)
+    plain(0, 1)
+    plain(0, 2)
+    passing(0, 0, 0)
+    passing(0, 0, 1)
+    project(1, 3)
+    passing(0, 1, 0)
+    passing(0, 1, 1)
     project(1, 6)
-    arrive(0, 2, 2, 0)
-    arrive(0, 2, 2, 1)
     project(1, 7)
-    arrive(1, 2, 2, 0)
-    arrive(1, 2, 2, 1)
-    project(0, 8)
-    state_load.wait()
-    retain(0)
-    retain(1)
-    share_stats(0)
     project(1, 8)
     retain(2)
     retain(3)
     share_stats(1)
-    gate(0)
+    passing(0, 2, 0)
+    passing(0, 2, 1)
+    plain(0, 3)
+    passing(0, 3, 0)
+    passing(0, 3, 1)
+    row_far(0, 0)
+    row_far(0, 1)
     gate(1)
-    gate_copy(0, 1 - core).wait_recv()
-    plain(0, 0)
-    plain(0, 1)
-    plain(0, 2)
-    far(0, 0)
+    row_plain(0, 0)
+    row_plain(0, 1)
     gate_copy(1, 1 - core).wait_recv()
+    far(1, 0)
+    far(1, 1)
+    far(1, 2)
+    far(1, 3)
+    row_own(0, 0)
+    row_own(0, 1)
     plain(1, 0)
     plain(1, 1)
     plain(1, 2)
-    far(1, 0)
-    plain(0, 3)
-    plain(1, 3)
-    far(0, 1)
-    far(1, 1)
-    passing(0, 0, 0)
-    passing(0, 0, 1)
-    far(0, 2)
-    far(1, 2)
-    far(0, 3)
-    far(1, 3)
     passing(1, 0, 0)
     passing(1, 0, 1)
-    passing(0, 1, 0)
-    passing(0, 1, 1)
+    plain(1, 3)
     passing(1, 1, 0)
     passing(1, 1, 1)
-    row_far(0, 0)
-    row_far(0, 1)
-    passing(0, 2, 0)
-    passing(0, 2, 1)
+    row_passing(0, 0)
+    row_passing(0, 1)
     passing(1, 2, 0)
     passing(1, 2, 1)
-    passing(0, 3, 0)
-    passing(0, 3, 1)
     passing(1, 3, 0)
     passing(1, 3, 1)
+    finish(0, 0)
+    finish(0, 1)
     row_far(1, 0)
     row_far(1, 1)
-    row_passing(0, 0)
-    row_plain(0, 0)
     row_plain(1, 0)
-    row_passing(0, 1)
-    row_plain(0, 1)
+    row_plain(1, 1)
     row_passing(1, 0)
     row_passing(1, 1)
-    row_plain(1, 1)
-    row_own(0, 1)
-    row_own(0, 0)
     row_own(1, 1)
-    finish(0, 1)
-    finish(0, 0)
     row_own(1, 0)
+    finish(1, 0)
     finish(1, 1)
-    finish(1, 0)
 
     for sem, slots in enumerate((held.at[pl.ds(0, 2 * CHIPS - 1)], s1, s2, stats, gated.at[core])):
         remote(slots, slots, send_sems.at[sem], stat_sems.at[0], partner).wait_send()

time: 64.7 us -> 62.6 us (0.968)
  Pallas kernels: 63.8 us -> 61.7 us
    pallas_call x1, Pallas kernels: 60.4 us -> 58.2 us  [per_device(): pl.pallas_call(kernel, out_shape=(pltpu.VMEM((rows, BLOCK), BF16), pltpu....]
where the time goes in v5:
time: 62.6 us; the launch traced here: 62.5 us
  Pallas kernels  61.7 us (99%)
  between operations  0.8 us (1%)
    pallas_call x1, Pallas kernels, per_device(): pl.pallas_call(kernel, out_shape=(pltpu.VMEM((rows, BLOCK), BF16), pltpu....  58.2 us
    pallas_call x1, Pallas kernels, store(): pl.pallas_call(store_kernel, out_shape=(jax.ShapeDtypeStruct(out.shape, o...  3.46 us

profile of v5, /device:TPU:0, one launch (start us, length us, event | category | flops | bytes accessed | tf_op | source)
XLA Modules:
  0.0 62.5 jit_solution(4675730053590736633)
XLA Ops:
  0.6 58.2 %retention_step.1 = (bf16[1024,128]{1,0:T(8,128)(2,1)S(1)}, f32[32,256,256]{2,1,0:T(8,128)S(1)}) custom-call(bf16[1024,128]{1,0:T(8,128)(2,1)} %tokens.1, f32[16,1024]{1,0:T(8,128)} %bitcast.2, f32[1,256]{1,0:T(1,128)} %bitcast.3, f32[32,256,256]{2,1,0:T(8,128)} %state.1, bf16[4096,128]{1,0:T(8,128)(2,1)} %w_query.1, bf16[4096,128]{1,0:T(8,128)(2,1)} %w_key.1, ...), custom_call_target="tpu_custom_call" | custom-call | tf_op jit(solution)/shard_map/retention_step/pallas_call | solution.py:581
  58.8 3.5 %store.1 = (bf16[1024,128]{1,0:T(8,128)(2,1)}, f32[32,256,256]{2,1,0:T(8,128)}) custom-call(bf16[1024,128]{1,0:T(8,128)(2,1)S(1)} %get-tuple-element.4.out_in, f32[32,256,256]{2,1,0:T(8,128)S(1)} %get-tuple-element.5.state_in), custom_call_target="tpu_custom_call" | custom-call | tf_op jit(solution)/shard_map/store/pallas_call | solution.py:563
